TPU v7x, 256 devices: a whole 4x4x8 slice. The times are simulated.
256 devices in a mesh: agents: 64 (over z, x, core), group: 4 (over y).
Axes of the slice: x: 4, y: 4, z: 8, core: 2. Of those that a mesh axis runs over, the one named last changes fastest.
Arguments:
- q_lin: float32 [4, 40, 16384], P('group', None, 'agents'), may hold values from -6 to 6
- inverse: bfloat16 [4, 40, 40, 16384], P('group', None, None, 'agents'), may hold values from -0.5 to 1, as said below
- predict: bfloat16 [4, 40, 40, 16384], P('group', None, None, 'agents'), may hold values from -1 to 1
- free_traj: float32 [4, 40, 16384], P('group', None, 'agents'), may hold values from -6 to 6
- offsets: float32 [4, 8, 40, 16384], P('group', None, None, 'agents'), may hold values from -4 to 4
- multipliers: float32 [4, 8, 40, 16384], P('group', None, None, 'agents'), may hold values from -4 to 4
- nbr_owner: int32 [4, 8, 16384], P('group', None, 'agents'), may hold values from 0 to 63, as said below
- nbr_slot: int32 [4, 8, 16384], P('group', None, 'agents'), may hold values from -1 to 255
- platoon: int32 [4, 16384], P('group', 'agents'), may hold values from 0 to 127, as said below
Outputs:
- inputs_plan: float32 [4, 40, 16384], P('group', None, 'agents')
- multipliers_out: float32 [4, 8, 40, 16384], P('group', None, None, 'agents')
Inputs may be any that keep to these rules, and one draw needn't show every extreme that they name: `nbr_owner`: an agent's own block index is its row in the region // 256; each neighbour's owner lies within 2 blocks of it, slot 0 is never padded. `inverse`: symmetric for every agent. `platoon`: 32 or more platoons hold no agent of any region.
All inputs are finite; a program needn't handle non-finite values. Where the computation divides by a largest or mean magnitude, that divisor is 1e-20 or more.
Results may differ from a plain program's by a relative error of at most 0.0003.
Values sent between devices are 32-bit elements; how exact they have to be, the bound alone decides.
No kernel may reach another device: no remote copies, remote signals or barrier semaphores. Data moves between devices by JAX's collectives and lax.ppermute only.
A program may use at most 64 MiB of HBM per device.

v0:
```python
import functools

import jax
import jax.numpy as jnp
from jax import lax
from jax.sharding import Mesh
from jax.sharding import PartitionSpec as P

SPAN = 2
NPLAT = 128
ITERS = 3
AGENTS = ("agents_0", "agents_1", "agents_2")
AGENTS_GROUP = ("agents_0", "agents_1", "agents_2", "group")


RHO = 0.5
KAPPA = 0.5


def shifted(value, axis, steps):
    count = lax.axis_size(axis)
    first, last = (max(0, -steps), min(count, count - steps))
    return lax.ppermute(value, axis, [(source, source + steps) for source in range(first, last)])


def over_axes(x, axes):
    return functools.reduce(lax.psum, axes, x)


def all_in_one(x, axis):
    leaves = jax.tree.leaves(x)
    sequence = sorted(range(len(leaves)), key=lambda k: -leaves[k].size)
    width = (1, *leaves[sequence[0]].shape)[-1]
    lines = [
        jnp.pad(leaves[k].reshape(-1), (0, -leaves[k].size % width)).reshape(-1, width)
        for k in sequence
    ]
    both, at, found = (lax.all_gather(jnp.concatenate(lines), axis), 0, {})
    for k, line in zip(sequence, lines):
        section = both[:, at : at + len(line)].reshape(len(both), -1)
        found[k] = section[:, : leaves[k].size].reshape(-1, *leaves[k].shape)
        at += len(line)
    numbers = iter(range(len(leaves)))
    return jax.tree.map(lambda _: found[next(numbers)], x)


def once_a_type(x, axis):
    leaves, found = (jax.tree.leaves(x), {})
    for first, a in enumerate(leaves):
        if first not in found:
            alike = [k for k, b in enumerate(leaves) if b.dtype == a.dtype]
            got = (
                all_in_one([leaves[k] for k in alike], axis)
                if len(alike) > 1
                else [lax.all_gather(a, axis)]
            )
            for k, b in zip(alike, got):
                found[k] = b
    numbers = iter(range(len(leaves)))
    return jax.tree.map(lambda _: found[next(numbers)], x)


def joined_all(x, axes, combine):
    for axis in axes:
        pieces = once_a_type(x, axis)
        x = jax.tree.map(lambda part: part[0], pieces)
        for k in range(1, lax.axis_size(axis)):
            x = combine(x, jax.tree.map(lambda part: part[k], pieces))
    return x


def by_axis(x, axes):
    return functools.reduce(lax.pmax, axes, x)


def combine_stats(first, second):
    return (first[0] + second[0], jnp.maximum(first[1], second[1]))


def local(q_lin, inverse, predict, free_traj, offsets, multipliers, nbr_owner, nbr_slot, platoon):
    block = q_lin.shape[2]
    traj_len = free_traj.shape[1]
    alive = nbr_slot >= 0
    live = alive.astype(jnp.float32)[:, :, None, :]
    onehot = (platoon[:, None, :] == jnp.arange(NPLAT, dtype=jnp.int32)[None, :, None]).astype(
        jnp.float32
    )
    counts_local = jnp.sum(onehot, axis=(0, 2))
    mine = lax.axis_index(AGENTS)
    column = (nbr_owner - mine + SPAN) * block + nbr_slot
    column = jnp.where(alive, column, 0)[0].reshape(-1)

    def lookup(field):
        pieces = []
        for distance in range(-SPAN, SPAN + 1):
            if distance == 0:
                pieces.append(field)
            else:
                pieces.append(shifted(field, AGENTS, -distance))
        joined = jnp.concatenate(pieces, axis=2)
        taken = jnp.take(joined[0], column, axis=1).reshape(traj_len, nbr_slot.shape[1], block)
        return jnp.transpose(taken, (1, 0, 2))[None] * live

    def platoon_local(field):
        return jnp.einsum("rta,rpa->tp", field, onehot, precision=lax.Precision.HIGHEST)

    traj = free_traj
    lam = multipliers
    near = lookup(traj)
    sums, counts = (
        over_axes(platoon_local(traj), AGENTS_GROUP),
        over_axes(counts_local, AGENTS_GROUP),
    )
    divisor = jnp.maximum(counts, 1.0)[None, :]

    def spread(totals):
        means = totals / divisor
        return jnp.einsum("tp,rpa->rta", means, onehot, precision=lax.Precision.HIGHEST)

    attract = spread(sums)
    plan = jnp.zeros_like(q_lin)
    for step in range(ITERS):
        coupling = jnp.sum(live * (lam - RHO * (near + offsets)), axis=1) - KAPPA * attract
        rhs = q_lin + jnp.einsum(
            "rtja,rta->rja", predict.astype(jnp.float32), coupling, precision=lax.Precision.HIGHEST
        )
        plan = -jnp.einsum(
            "rija,rja->ria", inverse.astype(jnp.float32), rhs, precision=lax.Precision.HIGHEST
        )
        traj = (
            jnp.einsum(
                "rtja,rja->rta", predict.astype(jnp.float32), plan, precision=lax.Precision.HIGHEST
            )
            + free_traj
        )
        near = lookup(traj)
        gap = live * (traj[:, None] - near - offsets)
        local_peak = jnp.max(jnp.abs(gap))
        more = step + 1 < ITERS
        if more:
            sums, peak = joined_all((platoon_local(traj), local_peak), AGENTS_GROUP, combine_stats)
        else:
            peak = by_axis(local_peak, AGENTS_GROUP)
        lam = lam + gap / (1.0 + peak)
        if more:
            attract = spread(sums)
    return (plan, lam)


def solution(mesh):
    finer = Mesh(
        mesh.devices.reshape(8, 4, 2, mesh.shape["group"]),
        ("agents_0", "agents_1", "agents_2", "group"),
    )
    placed = (
        P("group", None, AGENTS),
        P("group", None, None, AGENTS),
        P("group", None, None, AGENTS),
        P("group", None, AGENTS),
        P("group", None, None, AGENTS),
        P("group", None, None, AGENTS),
        P("group", None, AGENTS),
        P("group", None, AGENTS),
        P("group", AGENTS),
    )
    return jax.shard_map(
        local,
        mesh=finer,
        in_specs=placed,
        out_specs=(P("group", None, AGENTS), P("group", None, None, AGENTS)),
        check_vma=False,
    )
```

profile of v0, /device:TPU:1, one launch (start us, length us, event | category | flops | bytes accessed | tf_op | source)
XLA Modules:
  0.0 351.5 jit_solution(14953525643626272424)
XLA Ops:
  4.6 4.0 %collective-permute-start.1 = (f32[1,40,256]{2,1,0:T(8,128)}, f32[1,40,256]{2,1,0:T(8,128)S(1)}, u32[]{:S(2)}, u32[]{:S(2)}) collective-permute-start(f32[1,40,256]{2,1,0:T(8,128)} %param.14), channel_id=1, source_target_pairs={{0,4},{4,8},{8,12},{12,16},{16,20},{20,24},{24,28},{28,32},{32,36}... | collective-permute-start | bytes 122888 | tf_op jit(solution)/shard_map/ppermute | solution.py:23
  15.0 28.5 %all-reduce.8 = (f32[40,128]{1,0:T(8,128)S(1)}, f32[128]{0:T(128)S(1)}) all-reduce(f32[40,128]{1,0:T(8,128)S(1)} %convolution_bitcast_fusion, f32[128]{0:T(128)S(1)} %convert_reduce_fusion), channel_id=1, replica_groups=mesh['agents_0'=8,'agents_1'=4,'agents_2'=2,'group'=4] {'agents_0'}, use_global_device_ids=true, to_apply=%region_1.3 | all-reduce | flops 5248 | bytes 41984 | tf_op jit(solution)/shard_map/psum | solution.py:27
  43.6 10.9 %all-reduce.10 = (f32[40,128]{1,0:T(8,128)S(1)}, f32[128]{0:T(128)S(1)}) all-reduce(f32[40,128]{1,0:T(8,128)S(1)} %get-tuple-element.3, f32[128]{0:T(128)S(1)} %get-tuple-element.4), channel_id=1, replica_groups=mesh['agents_0'=8,'agents_1'=4,'agents_2'=2,'group'=4] {'agents_1'}, use_global_device_ids=true, to_apply=%region_2.4 | all-reduce | flops 5248 | bytes 41984 | tf_op jit(solution)/shard_map/psum | solution.py:27
  54.5 16.2 %all-reduce.11 = (f32[40,128]{1,0:T(8,128)S(1)}, f32[128]{0:T(128)S(1)}) all-reduce(f32[40,128]{1,0:T(8,128)S(1)} %get-tuple-element.7, f32[128]{0:T(128)S(1)} %get-tuple-element.8), channel_id=1, replica_groups=mesh['agents_0'=8,'agents_1'=4,'agents_2'=2,'group'=4] {'agents_2'}, use_global_device_ids=true, to_apply=%region_3.5 | all-reduce | flops 5248 | bytes 41984 | tf_op jit(solution)/shard_map/psum | solution.py:27
  70.7 13.5 %all-reduce.9 = (f32[40,128]{1,0:T(8,128)S(1)}, f32[128]{0:T(128)S(1)}) all-reduce(f32[40,128]{1,0:T(8,128)S(1)} %get-tuple-element.9, f32[128]{0:T(128)S(1)} %get-tuple-element.10), channel_id=1, replica_groups=mesh['agents_0'=8,'agents_1'=4,'agents_2'=2,'group'=4] {'group'}, use_global_device_ids=true, to_apply=%region_4.6 | all-reduce | flops 5248 | bytes 41984 | tf_op jit(solution)/shard_map/psum | solution.py:27
  85.4 5.5 %gather_fusion = f32[2048,40]{1,0:T(8,128)S(1)} fusion(f32[40,1280]{0,1:T(8,128)S(1)} %bitcast.324, s32[2048]{0:T(1024)S(1)} %fusion.63), kind=kCustom, calls=%fused_computation.clone | custom fusion | bytes 663552 | tf_op jit(solution)/shard_map/jit(_take)/gather | solution.py:101
  95.6 7.5 %collective-permute-start.5 = (f32[1,40,256]{2,1,0:T(8,128)S(1)}, f32[1,40,256]{2,1,0:T(8,128)S(1)}, u32[]{:S(2)}, u32[]{:S(2)}) collective-permute-start(f32[1,40,256]{2,1,0:T(8,128)S(1)} %bitcast_add_fusion.7), channel_id=1, source_target_pairs={{0,4},{4,8},{8,12},{12,16},{16,20},{20,24},{24,28},{28,32},{32,36}... | collective-permute-start | bytes 122888 | tf_op jit(solution)/shard_map/ppermute | solution.py:23
  110.0 7.6 %gather_fusion.1 = f32[2048,40]{1,0:T(8,128)} fusion(f32[40,1280]{0,1:T(8,128)S(1)} %bitcast.325, s32[2048]{0:T(1024)S(1)} %fusion.63), kind=kCustom, calls=%fused_computation.1.clone | custom fusion | bytes 663552 | tf_op jit(solution)/shard_map/jit(_take)/gather | solution.py:101
  120.8 19.2 %all-gather.8 = f32[8,41,128]{2,1,0:T(8,128)S(1)} all-gather(f32[1,41,128]{2,1,0:T(8,128)S(1)} %maximum_bitcast_fusion), channel_id=2, replica_groups=mesh['agents_0'=8,'agents_1'=4,'agents_2'=2,'group'=4] {'agents_0'}, dimensions={0}, use_global_device_ids=true | all-gather | bytes 188928 | tf_op jit(solution)/shard_map/all_gather | solution.py:38
  145.7 9.1 %all-gather.9 = f32[4,41,128]{2,1,0:T(8,128)S(1)} all-gather(f32[1,41,128]{2,1,0:T(8,128)S(1)} %maximum_bitcast_fusion.1), channel_id=3, replica_groups=mesh['agents_0'=8,'agents_1'=4,'agents_2'=2,'group'=4] {'agents_1'}, dimensions={0}, use_global_device_ids=true | all-gather | bytes 104960 | tf_op jit(solution)/shard_map/all_gather | solution.py:38
  158.0 13.0 %all-gather.10 = f32[2,41,128]{2,1,0:T(8,128)S(1)} all-gather(f32[1,41,128]{2,1,0:T(8,128)S(1)} %maximum_bitcast_fusion.2), channel_id=4, replica_groups=mesh['agents_0'=8,'agents_1'=4,'agents_2'=2,'group'=4] {'agents_2'}, dimensions={0}, use_global_device_ids=true | all-gather | bytes 62976 | tf_op jit(solution)/shard_map/all_gather | solution.py:38
  172.9 9.0 %all-gather.11 = f32[4,41,128]{2,1,0:T(8,128)S(1)} all-gather(f32[1,41,128]{2,1,0:T(8,128)S(1)} %maximum_bitcast_fusion.3), channel_id=5, replica_groups=mesh['agents_0'=8,'agents_1'=4,'agents_2'=2,'group'=4] {'group'}, dimensions={0}, use_global_device_ids=true | all-gather | bytes 104960 | tf_op jit(solution)/shard_map/all_gather | solution.py:38
  189.9 5.0 %collective-permute-start.9 = (f32[1,40,256]{2,1,0:T(8,128)S(1)}, f32[1,40,256]{2,1,0:T(8,128)S(1)}, u32[]{:S(2)}, u32[]{:S(2)}) collective-permute-start(f32[1,40,256]{2,1,0:T(8,128)S(1)} %bitcast_add_fusion.5), channel_id=1, source_target_pairs={{0,4},{4,8},{8,12},{12,16},{16,20},{20,24},{24,28},{28,32},{32,36}... | collective-permute-start | bytes 122888 | tf_op jit(solution)/shard_map/ppermute | solution.py:23
  202.9 7.6 %gather_fusion.2 = f32[2048,40]{1,0:T(8,128)} fusion(f32[40,1280]{0,1:T(8,128)S(1)} %bitcast.326, s32[2048]{0:T(1024)S(1)} %fusion.63), kind=kCustom, calls=%fused_computation.2.clone | custom fusion | bytes 663552 | tf_op jit(solution)/shard_map/jit(_take)/gather | solution.py:101
  215.6 20.7 %all-gather.12 = f32[8,41,128]{2,1,0:T(8,128)S(1)} all-gather(f32[1,41,128]{2,1,0:T(8,128)S(1)} %maximum_bitcast_fusion.4), channel_id=6, replica_groups=mesh['agents_0'=8,'agents_1'=4,'agents_2'=2,'group'=4] {'agents_0'}, dimensions={0}, use_global_device_ids=true | all-gather | bytes 188928 | tf_op jit(solution)/shard_map/all_gather | solution.py:38
  241.9 10.2 %all-gather.13 = f32[4,41,128]{2,1,0:T(8,128)S(1)} all-gather(f32[1,41,128]{2,1,0:T(8,128)S(1)} %maximum_bitcast_fusion.5), channel_id=7, replica_groups=mesh['agents_0'=8,'agents_1'=4,'agents_2'=2,'group'=4] {'agents_1'}, dimensions={0}, use_global_device_ids=true | all-gather | bytes 104960 | tf_op jit(solution)/shard_map/all_gather | solution.py:38
  255.3 12.3 %all-gather.14 = f32[2,41,128]{2,1,0:T(8,128)S(1)} all-gather(f32[1,41,128]{2,1,0:T(8,128)S(1)} %maximum_bitcast_fusion.6), channel_id=8, replica_groups=mesh['agents_0'=8,'agents_1'=4,'agents_2'=2,'group'=4] {'agents_2'}, dimensions={0}, use_global_device_ids=true | all-gather | bytes 62976 | tf_op jit(solution)/shard_map/all_gather | solution.py:38
  269.5 9.0 %all-gather.15 = f32[4,41,128]{2,1,0:T(8,128)S(1)} all-gather(f32[1,41,128]{2,1,0:T(8,128)S(1)} %maximum_bitcast_fusion.7), channel_id=9, replica_groups=mesh['agents_0'=8,'agents_1'=4,'agents_2'=2,'group'=4] {'group'}, dimensions={0}, use_global_device_ids=true | all-gather | bytes 104960 | tf_op jit(solution)/shard_map/all_gather | solution.py:38
  287.1 5.1 %collective-permute-start.13 = (f32[1,40,256]{2,1,0:T(8,128)S(1)}, f32[1,40,256]{2,1,0:T(8,128)S(1)}, u32[]{:S(2)}, u32[]{:S(2)}) collective-permute-start(f32[1,40,256]{2,1,0:T(8,128)S(1)} %bitcast_add_fusion.3), channel_id=1, source_target_pairs={{0,4},{4,8},{8,12},{12,16},{16,20},{20,24},{24,28},{28,32},{32,36}... | collective-permute-start | bytes 122888 | tf_op jit(solution)/shard_map/ppermute | solution.py:23
  300.2 5.5 %gather_fusion.3 = f32[2048,40]{1,0:T(8,128)S(1)} fusion(f32[40,1280]{0,1:T(8,128)S(1)} %bitcast.323, s32[2048]{0:T(1024)S(1)} %fusion.63), kind=kCustom, calls=%fused_computation.3.clone | custom fusion | bytes 663552 | tf_op jit(solution)/shard_map/jit(_take)/gather | solution.py:101
  307.1 14.2 %pmax.28 = f32[]{:T(128)} all-reduce(f32[]{:T(128)} %abs_reduce_fusion), channel_id=1, replica_groups=mesh['agents_0'=8,'agents_1'=4,'agents_2'=2,'group'=4] {'agents_0'}, use_global_device_ids=true, to_apply=%region_15.17 | all-reduce | flops 1 | bytes 8 | tf_op jit(solution)/shard_map/pmax | solution.py:73
  321.3 11.0 %pmax.29 = f32[]{:T(128)} all-reduce(f32[]{:T(128)} %pmax.28), channel_id=1, replica_groups=mesh['agents_0'=8,'agents_1'=4,'agents_2'=2,'group'=4] {'agents_1'}, use_global_device_ids=true, to_apply=%region_16.18 | all-reduce | flops 1 | bytes 8 | tf_op jit(solution)/shard_map/pmax | solution.py:73
  332.2 10.9 %pmax.30 = f32[]{:T(128)} all-reduce(f32[]{:T(128)} %pmax.29), channel_id=1, replica_groups=mesh['agents_0'=8,'agents_1'=4,'agents_2'=2,'group'=4] {'agents_2'}, use_global_device_ids=true, to_apply=%region_17.19 | all-reduce | flops 1 | bytes 8 | tf_op jit(solution)/shard_map/pmax | solution.py:73
  343.2 6.8 %pmax.31 = f32[]{:T(128)} all-reduce(f32[]{:T(128)} %pmax.30), channel_id=1, replica_groups=mesh['agents_0'=8,'agents_1'=4,'agents_2'=2,'group'=4] {'group'}, use_global_device_ids=true, to_apply=%region_18.20 | all-reduce | flops 1 | bytes 8 | tf_op jit(solution)/shard_map/pmax | solution.py:73
  (162 shorter events, 64.2 us)
Async XLA Ops:
  0.6 83.6 %collective-permute-start = (f32[1,40,256]{2,1,0:T(8,128)}, f32[1,40,256]{2,1,0:T(8,128)S(1)}, u32[]{:S(2)}, u32[]{:S(2)}) collective-permute-start(f32[1,40,256]{2,1,0:T(8,128)} %param.14), channel_id=1, source_target_pairs={{0,8},{4,12},{8,16},{12,20},{16,24},{20,28},{24,32},{28,36},{32,40... | collective-permute-start | bytes 122888 | tf_op jit(solution)/shard_map/ppermute | solution.py:23
  4.6 79.7 %collective-permute-start.1 = (f32[1,40,256]{2,1,0:T(8,128)}, f32[1,40,256]{2,1,0:T(8,128)S(1)}, u32[]{:S(2)}, u32[]{:S(2)}) collective-permute-start(f32[1,40,256]{2,1,0:T(8,128)} %param.14), channel_id=1, source_target_pairs={{0,4},{4,8},{8,12},{12,16},{16,20},{20,24},{24,28},{28,32},{32,36}... | collective-permute-start | bytes 122888 | tf_op jit(solution)/shard_map/ppermute | solution.py:23
  8.5 76.5 %collective-permute-start.2 = (f32[1,40,256]{2,1,0:T(8,128)}, f32[1,40,256]{2,1,0:T(8,128)S(1)}, u32[]{:S(2)}, u32[]{:S(2)}) collective-permute-start(f32[1,40,256]{2,1,0:T(8,128)} %param.14), channel_id=1, source_target_pairs={{4,0},{8,4},{12,8},{16,12},{20,16},{24,20},{28,24},{32,28},{36,32}... | collective-permute-start | bytes 122888 | tf_op jit(solution)/shard_map/ppermute | solution.py:23
  10.5 74.6 %collective-permute-start.3 = (f32[1,40,256]{2,1,0:T(8,128)}, f32[1,40,256]{2,1,0:T(8,128)S(1)}, u32[]{:S(2)}, u32[]{:S(2)}) collective-permute-start(f32[1,40,256]{2,1,0:T(8,128)} %param.14), channel_id=1, source_target_pairs={{8,0},{12,4},{16,8},{20,12},{24,16},{28,20},{32,24},{36,28},{40,32... | collective-permute-start | bytes 122888 | tf_op jit(solution)/shard_map/ppermute | solution.py:23
  91.2 1.1 copy-start.3
  91.2 1.1 copy-start.10
  91.2 1.3 copy-start
  92.3 1.2 copy-start.2
  94.3 12.2 %collective-permute-start.4 = (f32[1,40,256]{2,1,0:T(8,128)S(1)}, f32[1,40,256]{2,1,0:T(8,128)S(1)}, u32[]{:S(2)}, u32[]{:S(2)}) collective-permute-start(f32[1,40,256]{2,1,0:T(8,128)S(1)} %bitcast_add_fusion.7), channel_id=1, source_target_pairs={{0,8},{4,12},{8,16},{12,20},{16,24},{20,28},{24,32},{28,36},{32,40... | collective-permute-start | bytes 122888 | tf_op jit(solution)/shard_map/ppermute | solution.py:23
  95.6 10.9 %collective-permute-start.5 = (f32[1,40,256]{2,1,0:T(8,128)S(1)}, f32[1,40,256]{2,1,0:T(8,128)S(1)}, u32[]{:S(2)}, u32[]{:S(2)}) collective-permute-start(f32[1,40,256]{2,1,0:T(8,128)S(1)} %bitcast_add_fusion.7), channel_id=1, source_target_pairs={{0,4},{4,8},{8,12},{12,16},{16,20},{20,24},{24,28},{28,32},{32,36}... | collective-permute-start | bytes 122888 | tf_op jit(solution)/shard_map/ppermute | solution.py:23
  103.0 5.3 %collective-permute-start.6 = (f32[1,40,256]{2,1,0:T(8,128)S(1)}, f32[1,40,256]{2,1,0:T(8,128)S(1)}, u32[]{:S(2)}, u32[]{:S(2)}) collective-permute-start(f32[1,40,256]{2,1,0:T(8,128)S(1)} %bitcast_add_fusion.7), channel_id=1, source_target_pairs={{4,0},{8,4},{12,8},{16,12},{20,16},{24,20},{28,24},{32,28},{36,32}... | collective-permute-start | bytes 122888 | tf_op jit(solution)/shard_map/ppermute | solution.py:23
  105.0 4.7 %collective-permute-start.7 = (f32[1,40,256]{2,1,0:T(8,128)S(1)}, f32[1,40,256]{2,1,0:T(8,128)S(1)}, u32[]{:S(2)}, u32[]{:S(2)}) collective-permute-start(f32[1,40,256]{2,1,0:T(8,128)S(1)} %bitcast_add_fusion.7), channel_id=1, source_target_pairs={{8,0},{12,4},{16,8},{20,12},{24,16},{28,20},{32,24},{36,28},{40,32... | collective-permute-start | bytes 122888 | tf_op jit(solution)/shard_map/ppermute | solution.py:23
  119.4 65.7 %copy-start.4 = (f32[1,8,40,256]{3,2,1,0:T(8,128)S(1)}, f32[1,8,40,256]{3,2,1,0:T(8,128)}, u32[]{:S(2)}) copy-start(f32[1,8,40,256]{3,2,1,0:T(8,128)} %param.16) | copy-start | bytes 983044
  186.3 12.1 %collective-permute-start.8 = (f32[1,40,256]{2,1,0:T(8,128)S(1)}, f32[1,40,256]{2,1,0:T(8,128)S(1)}, u32[]{:S(2)}, u32[]{:S(2)}) collective-permute-start(f32[1,40,256]{2,1,0:T(8,128)S(1)} %bitcast_add_fusion.5), channel_id=1, source_target_pairs={{0,8},{4,12},{8,16},{12,20},{16,24},{20,28},{24,32},{28,36},{32,40... | collective-permute-start | bytes 122888 | tf_op jit(solution)/shard_map/ppermute | solution.py:23
  189.9 8.5 %collective-permute-start.9 = (f32[1,40,256]{2,1,0:T(8,128)S(1)}, f32[1,40,256]{2,1,0:T(8,128)S(1)}, u32[]{:S(2)}, u32[]{:S(2)}) collective-permute-start(f32[1,40,256]{2,1,0:T(8,128)S(1)} %bitcast_add_fusion.5), channel_id=1, source_target_pairs={{0,4},{4,8},{8,12},{12,16},{16,20},{20,24},{24,28},{28,32},{32,36}... | collective-permute-start | bytes 122888 | tf_op jit(solution)/shard_map/ppermute | solution.py:23
  195.0 5.3 %collective-permute-start.10 = (f32[1,40,256]{2,1,0:T(8,128)S(1)}, f32[1,40,256]{2,1,0:T(8,128)S(1)}, u32[]{:S(2)}, u32[]{:S(2)}) collective-permute-start(f32[1,40,256]{2,1,0:T(8,128)S(1)} %bitcast_add_fusion.5), channel_id=1, source_target_pairs={{4,0},{8,4},{12,8},{16,12},{20,16},{24,20},{28,24},{32,28},{36,32}... | collective-permute-start | bytes 122888 | tf_op jit(solution)/shard_map/ppermute | solution.py:23
  196.9 5.8 %collective-permute-start.11 = (f32[1,40,256]{2,1,0:T(8,128)S(1)}, f32[1,40,256]{2,1,0:T(8,128)S(1)}, u32[]{:S(2)}, u32[]{:S(2)}) collective-permute-start(f32[1,40,256]{2,1,0:T(8,128)S(1)} %bitcast_add_fusion.5), channel_id=1, source_target_pairs={{8,0},{12,4},{16,8},{20,12},{24,16},{28,20},{32,24},{36,28},{40,32... | collective-permute-start | bytes 122888 | tf_op jit(solution)/shard_map/ppermute | solution.py:23
  213.1 68.6 %copy-start.5 = (f32[1,8,40,256]{3,2,1,0:T(8,128)S(1)}, f32[1,8,40,256]{3,2,1,0:T(8,128)}, u32[]{:S(2)}) copy-start(f32[1,8,40,256]{3,2,1,0:T(8,128)} %param.16) | copy-start | bytes 983044
  213.1 68.6 %copy-start.6 = (f32[40,8,256]{2,0,1:T(8,128)S(1)}, f32[40,8,256]{2,0,1:T(8,128)}, u32[]{:S(2)}) copy-start(f32[40,8,256]{2,0,1:T(8,128)} %copy.41) | copy-start | bytes 983044
  284.1 11.3 %collective-permute-start.12 = (f32[1,40,256]{2,1,0:T(8,128)S(1)}, f32[1,40,256]{2,1,0:T(8,128)S(1)}, u32[]{:S(2)}, u32[]{:S(2)}) collective-permute-start(f32[1,40,256]{2,1,0:T(8,128)S(1)} %bitcast_add_fusion.3), channel_id=1, source_target_pairs={{0,8},{4,12},{8,16},{12,20},{16,24},{20,28},{24,32},{28,36},{32,40... | collective-permute-start | bytes 122888 | tf_op jit(solution)/shard_map/ppermute | solution.py:23
  287.1 8.4 %collective-permute-start.13 = (f32[1,40,256]{2,1,0:T(8,128)S(1)}, f32[1,40,256]{2,1,0:T(8,128)S(1)}, u32[]{:S(2)}, u32[]{:S(2)}) collective-permute-start(f32[1,40,256]{2,1,0:T(8,128)S(1)} %bitcast_add_fusion.3), channel_id=1, source_target_pairs={{0,4},{4,8},{8,12},{12,16},{16,20},{20,24},{24,28},{28,32},{32,36}... | collective-permute-start | bytes 122888 | tf_op jit(solution)/shard_map/ppermute | solution.py:23
  292.2 5.3 %collective-permute-start.14 = (f32[1,40,256]{2,1,0:T(8,128)S(1)}, f32[1,40,256]{2,1,0:T(8,128)S(1)}, u32[]{:S(2)}, u32[]{:S(2)}) collective-permute-start(f32[1,40,256]{2,1,0:T(8,128)S(1)} %bitcast_add_fusion.3), channel_id=1, source_target_pairs={{4,0},{8,4},{12,8},{16,12},{20,16},{24,20},{28,24},{32,28},{36,32}... | collective-permute-start | bytes 122888 | tf_op jit(solution)/shard_map/ppermute | solution.py:23
  294.2 5.8 %collective-permute-start.15 = (f32[1,40,256]{2,1,0:T(8,128)S(1)}, f32[1,40,256]{2,1,0:T(8,128)S(1)}, u32[]{:S(2)}, u32[]{:S(2)}) collective-permute-start(f32[1,40,256]{2,1,0:T(8,128)S(1)} %bitcast_add_fusion.3), channel_id=1, source_target_pairs={{8,0},{12,4},{16,8},{20,12},{24,16},{28,20},{32,24},{36,28},{40,32... | collective-permute-start | bytes 122888 | tf_op jit(solution)/shard_map/ppermute | solution.py:23
  306.0 44.7 %copy-start.7 = (f32[1,8,40,256]{3,2,1,0:T(8,128)S(1)}, f32[1,8,40,256]{3,2,1,0:T(8,128)}, u32[]{:S(2)}) copy-start(f32[1,8,40,256]{3,2,1,0:T(8,128)} %get-tuple-element.12) | copy-start | bytes 983044
  (3 other events, 2.6 us)
where the time goes:
time: 354 us; the launch traced here: 351 us
  blocking collectives  215 us (61%)
  starting transfers between devices  46.2 us (13%)
  local copies, waits for them, and re-layouts  38 us (11%)
  between operations  24.9 us (7%)
  other arithmetic  13.9 us (4%)
  waiting for transfers between devices  11.8 us (3%)
    all_gather x8, blocking collectives, all_in_one(): both, at, found = (lax.all_gather(jnp.concatenate(lines), axis), 0, {})  103 us
    psum x4, blocking collectives, over_axes(): return functools.reduce(lax.psum, axes, x)  69.2 us
    ppermute x16, starting transfers between devices, shifted(): lax.ppermute(value, axis, [(source, source + steps) for source in range(f...  46.2 us
    pmax x4, blocking collectives, by_axis(): return functools.reduce(lax.pmax, axes, x)  42.9 us
    gather x4, local copies, waits for them, and re-layouts, lookup(): jnp.take(joined[0], column, axis=1)  26.1 us
    ppermute x16, waiting for transfers between devices, shifted(): lax.ppermute(value, axis, [(source, source + steps) for source in range(f...  11.8 us
  transfers between devices with their start and end apart: 16, of which 6 were waited for; matrix products, arithmetic and copies ran while one was open for 1% of the time, Pallas kernels for 0%

commit v1 on v0

--- a/solution.py
+++ b/solution.py
@@ -1,4 +1,5 @@
 import functools
+import itertools
 
 import jax
 import jax.numpy as jnp
@@ -23,58 +24,49 @@
     return lax.ppermute(value, axis, [(source, source + steps) for source in range(first, last)])
 
 
-def over_axes(x, axes):
-    return functools.reduce(lax.psum, axes, x)
+def exchanged(value, axes, sources):
+    sizes = [lax.axis_size(axis) for axis in axes]
+    places = list(itertools.product(*[range(size) for size in sizes]))
+    at = {place: k for k, place in enumerate(places)}
+    return [value] + [
+        lax.ppermute(value, axes, [(at[source(*place)], at[place]) for place in places])
+        for source in sources
+    ]
 
 
-def all_in_one(x, axis):
-    leaves = jax.tree.leaves(x)
-    sequence = sorted(range(len(leaves)), key=lambda k: -leaves[k].size)
-    width = (1, *leaves[sequence[0]].shape)[-1]
-    lines = [
-        jnp.pad(leaves[k].reshape(-1), (0, -leaves[k].size % width)).reshape(-1, width)
-        for k in sequence
-    ]
-    both, at, found = (lax.all_gather(jnp.concatenate(lines), axis), 0, {})
-    for k, line in zip(sequence, lines):
-        section = both[:, at : at + len(line)].reshape(len(both), -1)
-        found[k] = section[:, : leaves[k].size].reshape(-1, *leaves[k].shape)
-        at += len(line)
-    numbers = iter(range(len(leaves)))
-    return jax.tree.map(lambda _: found[next(numbers)], x)
+def ring(size):
+    return [lambda p, k=k: ((p + k) % size,) for k in range(1, size)]
 
 
-def once_a_type(x, axis):
-    leaves, found = (jax.tree.leaves(x), {})
-    for first, a in enumerate(leaves):
-        if first not in found:
-            alike = [k for k, b in enumerate(leaves) if b.dtype == a.dtype]
-            got = (
-                all_in_one([leaves[k] for k in alike], axis)
-                if len(alike) > 1
-                else [lax.all_gather(a, axis)]
-            )
-            for k, b in zip(alike, got):
-                found[k] = b
-    numbers = iter(range(len(leaves)))
-    return jax.tree.map(lambda _: found[next(numbers)], x)
+PAIRS = [lambda z, c: (z, 1 - c), lambda z, c: (z ^ 1, c), lambda z, c: (z ^ 1, 1 - c)]
+OTHERS = [
+    lambda z: ((z - 1 + 2 * (z % 2)) % 8,),
+    lambda z: ((z + 2 - 4 * (z % 2)) % 8,),
+    lambda z: (z ^ 5,),
+]
 
 
-def joined_all(x, axes, combine):
-    for axis in axes:
-        pieces = once_a_type(x, axis)
-        x = jax.tree.map(lambda part: part[0], pieces)
-        for k in range(1, lax.axis_size(axis)):
-            x = combine(x, jax.tree.map(lambda part: part[k], pieces))
-    return x
+def joined_all(value, combine):
+    stages = (
+        (("agents_0", "agents_2"), PAIRS),
+        (("agents_0",), OTHERS),
+        (("agents_1",), ring(4)),
+        (("group",), ring(4)),
+    )
+    for axes, sources in stages:
+        value = combine(exchanged(value, axes, sources))
+    return value
 
 
-def by_axis(x, axes):
-    return functools.reduce(lax.pmax, axes, x)
+def sum_and_peak(pieces):
+    row = lax.broadcasted_iota(jnp.int32, pieces[0].shape, 0)
+    return jnp.where(
+        row < pieces[0].shape[0] - 1, sum(pieces[1:], pieces[0]), functools.reduce(jnp.maximum, pieces)
+    )
 
 
-def combine_stats(first, second):
-    return (first[0] + second[0], jnp.maximum(first[1], second[1]))
+def added(pieces):
+    return sum(pieces[1:], pieces[0])
 
 
 def local(q_lin, inverse, predict, free_traj, offsets, multipliers, nbr_owner, nbr_slot, platoon):
@@ -107,10 +99,8 @@
     traj = free_traj
     lam = multipliers
     near = lookup(traj)
-    sums, counts = (
-        over_axes(platoon_local(traj), AGENTS_GROUP),
-        over_axes(counts_local, AGENTS_GROUP),
-    )
+    both = joined_all(jnp.concatenate([platoon_local(traj), counts_local[None]]), added)
+    sums, counts = both[:traj_len], both[traj_len]
     divisor = jnp.maximum(counts, 1.0)[None, :]
 
     def spread(totals):
@@ -138,9 +128,13 @@
         local_peak = jnp.max(jnp.abs(gap))
         more = step + 1 < ITERS
         if more:
-            sums, peak = joined_all((platoon_local(traj), local_peak), AGENTS_GROUP, combine_stats)
+            row = jnp.full((1, NPLAT), local_peak)
+            both = joined_all(jnp.concatenate([platoon_local(traj), row]), sum_and_peak)
+            sums, peak = both[:traj_len], both[traj_len, 0]
         else:
-            peak = by_axis(local_peak, AGENTS_GROUP)
+            count = lax.axis_size(AGENTS_GROUP)
+            every = jnp.full((count, NPLAT), local_peak)
+            peak = jnp.max(lax.all_to_all(every, AGENTS_GROUP, 0, 0, tiled=True))
         lam = lam + gap / (1.0 + peak)
         if more:
             attract = spread(sums)

time: 354 us -> 231 us (0.65)
  blocking collectives: 215 us -> 26.5 us
  starting transfers between devices: 46.2 us -> 102 us
  waiting for transfers between devices: 11.8 us -> 45.9 us
  between operations: 24.9 us -> 3.37 us
  local copies, waits for them, and re-layouts: 38 us -> 34.1 us
    all_gather x8 -> x0, blocking collectives: 103 us -> none  [all_in_one(): both, at, found = (lax.all_gather(jnp.concatenate(lines), axis), 0, {})]
    psum x4 -> x0, blocking collectives: 69.2 us -> none  [over_axes(): return functools.reduce(lax.psum, axes, x)]
    ppermute x0 -> x36, starting transfers between devices: none -> 53.1 us  [exchanged(): lax.ppermute(value, axes, [(at[source(*place)], at[place]) for place in p...]
    pmax x4 -> x0, blocking collectives: 42.9 us -> none  [by_axis(): return functools.reduce(lax.pmax, axes, x)]
    ppermute x0 -> x36, waiting for transfers between devices: none -> 36.2 us  [exchanged(): lax.ppermute(value, axes, [(at[source(*place)], at[place]) for place in p...]
    all_to_all x0 -> x1, blocking collectives: none -> 26.5 us  [local(): peak = jnp.max(lax.all_to_all(every, AGENTS_GROUP, 0, 0, tiled=True))]
    slice x16 -> x2, local copies, waits for them, and re-layouts: 4.81 us -> 1.09 us  [local(): sums, peak = (both[:traj_len], both[traj_len, 0])]
  transfers between devices with their start and end apart: 16 -> 52, of which waited for: 6 -> 28; matrix products, arithmetic and copies ran while one was open for 1% -> 5% of each run, Pallas kernels for 0% -> 0%
where the time goes in v1:
time: 231 us; the launch traced here: 230 us
  starting transfers between devices  102 us (44%)
  waiting for transfers between devices  45.9 us (20%)
  local copies, waits for them, and re-layouts  34.1 us (15%)
  blocking collectives  26.5 us (11%)
  other arithmetic  16.6 us (7%)
  between operations  3.37 us (1%)
    ppermute x36, starting transfers between devices, exchanged(): lax.ppermute(value, axes, [(at[source(*place)], at[place]) for place in p...  53.1 us
    ppermute x16, starting transfers between devices, shifted(): lax.ppermute(value, axis, [(source, source + steps) for source in range(f...  48.8 us
    ppermute x36, waiting for transfers between devices, exchanged(): lax.ppermute(value, axes, [(at[source(*place)], at[place]) for place in p...  36.2 us
    all_to_all x1, blocking collectives, local(): peak = jnp.max(lax.all_to_all(every, AGENTS_GROUP, 0, 0, tiled=True))  26.5 us
    gather x4, local copies, waits for them, and re-layouts, lookup(): jnp.take(joined[0], column, axis=1)  26.1 us
    ppermute x16, waiting for transfers between devices, shifted(): lax.ppermute(value, axis, [(source, source + steps) for source in range(f...  9.75 us
  transfers between devices with their start and end apart: 52, of which 28 were waited for; matrix products, arithmetic and copies ran while one was open for 5% of the time, Pallas kernels for 0%

profile of v1, /device:TPU:1, one launch (start us, length us, event | category | flops | bytes accessed | tf_op | source)
XLA Modules:
  0.0 230.4 jit_solution(14145813342877985465)
XLA Ops:
  2.4 3.3 %collective-permute-start.4 = (f32[41,128]{1,0:T(8,128)S(1)}, f32[41,128]{1,0:T(8,128)S(1)}, u32[]{:S(2)}, u32[]{:S(2)}) collective-permute-start(f32[41,128]{1,0:T(8,128)S(1)} %pad_maximum_fusion), channel_id=1, source_target_pairs={{4,0},{0,4},{36,32},{32,36},{68,64},{64,68},{100,96},{96,100},{132... | collective-permute-start | bytes 62984 | tf_op jit(solution)/shard_map/ppermute | solution.py:32
  8.9 3.6 %collective-permute-start.1 = (f32[1,40,256]{2,1,0:T(8,128)}, f32[1,40,256]{2,1,0:T(8,128)S(1)}, u32[]{:S(2)}, u32[]{:S(2)}) collective-permute-start(f32[1,40,256]{2,1,0:T(8,128)} %param.14), channel_id=1, source_target_pairs={{0,4},{4,8},{8,12},{12,16},{16,20},{20,24},{24,28},{28,32},{32,36}... | collective-permute-start | bytes 122888 | tf_op jit(solution)/shard_map/ppermute | solution.py:24
  17.2 8.5 %collective-permute-start.7 = (f32[41,128]{1,0:T(8,128)S(1)}, f32[41,128]{1,0:T(8,128)S(1)}, u32[]{:S(2)}, u32[]{:S(2)}) collective-permute-start(f32[41,128]{1,0:T(8,128)S(1)} %add_add_fusion.3), channel_id=1, source_target_pairs={{224,0},{64,32},{32,64},{128,96},{96,128},{192,160},{160,192},{0,2... | collective-permute-start | bytes 62984 | tf_op jit(solution)/shard_map/ppermute | solution.py:32
  28.9 5.5 %gather_fusion = f32[2048,40]{1,0:T(8,128)S(1)} fusion(f32[40,1280]{0,1:T(8,128)S(1)} %bitcast.260, s32[2048]{0:T(1024)S(1)} %fusion.48), kind=kCustom, calls=%fused_computation.clone | custom fusion | bytes 663552 | tf_op jit(solution)/shard_map/jit(_take)/gather | solution.py:93
  39.7 2.8 %collective-permute-start.13 = (f32[41,128]{1,0:T(8,128)S(1)}, f32[41,128]{1,0:T(8,128)S(1)}, u32[]{:S(2)}, u32[]{:S(2)}) collective-permute-start(f32[41,128]{1,0:T(8,128)S(1)} %add_add_fusion.1), channel_id=1, source_target_pairs={{1,0},{2,1},{3,2},{0,3},{5,4},{6,5},{7,6},{4,7},{9,8},{10,9},{11,1... | collective-permute-start | bytes 62984 | tf_op jit(solution)/shard_map/ppermute | solution.py:32
  48.2 2.5 %collective-permute-start.16 = (f32[1,40,256]{2,1,0:T(8,128)S(1)}, f32[1,40,256]{2,1,0:T(8,128)S(1)}, u32[]{:S(2)}, u32[]{:S(2)}) collective-permute-start(f32[1,40,256]{2,1,0:T(8,128)S(1)} %bitcast_add_fusion.7), channel_id=1, source_target_pairs={{0,8},{4,12},{8,16},{12,20},{16,24},{20,28},{24,32},{28,36},{32,40... | collective-permute-start | bytes 122888 | tf_op jit(solution)/shard_map/ppermute | solution.py:24
  50.7 7.7 %collective-permute-start.17 = (f32[1,40,256]{2,1,0:T(8,128)S(1)}, f32[1,40,256]{2,1,0:T(8,128)S(1)}, u32[]{:S(2)}, u32[]{:S(2)}) collective-permute-start(f32[1,40,256]{2,1,0:T(8,128)S(1)} %bitcast_add_fusion.7), channel_id=1, source_target_pairs={{0,4},{4,8},{8,12},{12,16},{16,20},{20,24},{24,28},{28,32},{32,36}... | collective-permute-start | bytes 122888 | tf_op jit(solution)/shard_map/ppermute | solution.py:24
  65.3 7.6 %gather_fusion.1 = f32[2048,40]{1,0:T(8,128)} fusion(f32[40,1280]{0,1:T(8,128)S(1)} %bitcast.261, s32[2048]{0:T(1024)S(1)} %fusion.48), kind=kCustom, calls=%fused_computation.1.clone | custom fusion | bytes 663552 | tf_op jit(solution)/shard_map/jit(_take)/gather | solution.py:93
  77.4 5.3 %collective-permute-start.21 = (f32[41,128]{1,0:T(8,128)S(1)}, f32[41,128]{1,0:T(8,128)S(1)}, u32[]{:S(2)}, u32[]{:S(2)}) collective-permute-start(f32[41,128]{1,0:T(8,128)S(1)} %concatenate.24), channel_id=1, source_target_pairs={{32,0},{36,4},{0,32},{4,36},{96,64},{100,68},{64,96},{68,100},{160... | collective-permute-start | bytes 62984 | tf_op jit(solution)/shard_map/ppermute | solution.py:32
  83.9 2.3 %collective-permute-done.22 = f32[41,128]{1,0:T(8,128)S(1)} collective-permute-done((f32[41,128]{1,0:T(8,128)S(1)}, f32[41,128]{1,0:T(8,128)S(1)}, u32[]{:S(2)}, u32[]{:S(2)}) %collective-permute-start.22) | collective-permute-done | bytes 21024 | tf_op jit(solution)/shard_map/ppermute | solution.py:32
  86.9 2.2 collective-permute-start.23
  89.2 3.6 %collective-permute-start.24 = (f32[41,128]{1,0:T(8,128)S(1)}, f32[41,128]{1,0:T(8,128)S(1)}, u32[]{:S(2)}, u32[]{:S(2)}) collective-permute-start(f32[41,128]{1,0:T(8,128)S(1)} %maximum_select_fusion.7), channel_id=1, source_target_pairs={{64,0},{224,32},{128,64},{32,96},{192,128},{96,160},{0,192},{160,2... | collective-permute-start | bytes 62984 | tf_op jit(solution)/shard_map/ppermute | solution.py:32
  93.7 4.7 %collective-permute-done.25 = f32[41,128]{1,0:T(8,128)S(1)} collective-permute-done((f32[41,128]{1,0:T(8,128)S(1)}, f32[41,128]{1,0:T(8,128)S(1)}, u32[]{:S(2)}, u32[]{:S(2)}) %collective-permute-start.25) | collective-permute-done | bytes 21024 | tf_op jit(solution)/shard_map/ppermute | solution.py:32
  101.2 2.7 %collective-permute-done.27 = f32[41,128]{1,0:T(8,128)S(1)} collective-permute-done((f32[41,128]{1,0:T(8,128)S(1)}, f32[41,128]{1,0:T(8,128)S(1)}, u32[]{:S(2)}, u32[]{:S(2)}) %collective-permute-start.27) | collective-permute-done | bytes 21024 | tf_op jit(solution)/shard_map/ppermute | solution.py:32
  114.1 8.1 %collective-permute-start.33 = (f32[1,40,256]{2,1,0:T(8,128)S(1)}, f32[1,40,256]{2,1,0:T(8,128)S(1)}, u32[]{:S(2)}, u32[]{:S(2)}) collective-permute-start(f32[1,40,256]{2,1,0:T(8,128)S(1)} %bitcast_add_fusion.5), channel_id=1, source_target_pairs={{0,4},{4,8},{8,12},{12,16},{16,20},{20,24},{24,28},{28,32},{32,36}... | collective-permute-start | bytes 122888 | tf_op jit(solution)/shard_map/ppermute | solution.py:24
  129.1 7.6 %gather_fusion.2 = f32[2048,40]{1,0:T(8,128)} fusion(f32[40,1280]{0,1:T(8,128)S(1)} %bitcast.262, s32[2048]{0:T(1024)S(1)} %fusion.48), kind=kCustom, calls=%fused_computation.2.clone | custom fusion | bytes 663552 | tf_op jit(solution)/shard_map/jit(_take)/gather | solution.py:93
  143.0 3.8 %collective-permute-start.37 = (f32[41,128]{1,0:T(8,128)S(1)}, f32[41,128]{1,0:T(8,128)S(1)}, u32[]{:S(2)}, u32[]{:S(2)}) collective-permute-start(f32[41,128]{1,0:T(8,128)S(1)} %concatenate.26), channel_id=1, source_target_pairs={{32,0},{36,4},{0,32},{4,36},{96,64},{100,68},{64,96},{68,100},{160... | collective-permute-start | bytes 62984 | tf_op jit(solution)/shard_map/ppermute | solution.py:32
  150.7 3.1 %collective-permute-start.39 = (f32[41,128]{1,0:T(8,128)S(1)}, f32[41,128]{1,0:T(8,128)S(1)}, u32[]{:S(2)}, u32[]{:S(2)}) collective-permute-start(f32[41,128]{1,0:T(8,128)S(1)} %maximum_select_fusion.3), channel_id=1, source_target_pairs={{224,0},{64,32},{32,64},{128,96},{96,128},{192,160},{160,192},{0,2... | collective-permute-start | bytes 62984 | tf_op jit(solution)/shard_map/ppermute | solution.py:32
  157.5 4.1 %collective-permute-done.41 = f32[41,128]{1,0:T(8,128)S(1)} collective-permute-done((f32[41,128]{1,0:T(8,128)S(1)}, f32[41,128]{1,0:T(8,128)S(1)}, u32[]{:S(2)}, u32[]{:S(2)}) %collective-permute-start.41) | collective-permute-done | bytes 21024 | tf_op jit(solution)/shard_map/ppermute | solution.py:32
  164.6 3.2 %collective-permute-done.43 = f32[41,128]{1,0:T(8,128)S(1)} collective-permute-done((f32[41,128]{1,0:T(8,128)S(1)}, f32[41,128]{1,0:T(8,128)S(1)}, u32[]{:S(2)}, u32[]{:S(2)}) %collective-permute-start.43) | collective-permute-done | bytes 21024 | tf_op jit(solution)/shard_map/ppermute | solution.py:32
  170.9 2.6 %collective-permute-done.46 = f32[41,128]{1,0:T(8,128)S(1)} collective-permute-done((f32[41,128]{1,0:T(8,128)S(1)}, f32[41,128]{1,0:T(8,128)S(1)}, u32[]{:S(2)}, u32[]{:S(2)}) %collective-permute-start.46) | collective-permute-done | bytes 21024 | tf_op jit(solution)/shard_map/ppermute | solution.py:32
  178.2 9.2 %collective-permute-start.49 = (f32[1,40,256]{2,1,0:T(8,128)S(1)}, f32[1,40,256]{2,1,0:T(8,128)S(1)}, u32[]{:S(2)}, u32[]{:S(2)}) collective-permute-start(f32[1,40,256]{2,1,0:T(8,128)S(1)} %bitcast_add_fusion.3), channel_id=1, source_target_pairs={{0,4},{4,8},{8,12},{12,16},{16,20},{20,24},{24,28},{28,32},{32,36}... | collective-permute-start | bytes 122888 | tf_op jit(solution)/shard_map/ppermute | solution.py:24
  194.3 5.5 %gather_fusion.3 = f32[2048,40]{1,0:T(8,128)S(1)} fusion(f32[40,1280]{0,1:T(8,128)S(1)} %bitcast.259, s32[2048]{0:T(1024)S(1)} %fusion.48), kind=kCustom, calls=%fused_computation.3.clone | custom fusion | bytes 663552 | tf_op jit(solution)/shard_map/jit(_take)/gather | solution.py:93
  201.8 26.5 %all_to_all.6 = f32[256,1,128]{2,1,0:T(1,128)S(1)} all-to-all(f32[256,1,128]{2,1,0:T(1,128)S(1)} %broadcast_in_dim.16), channel_id=1, replica_groups=mesh['agents_0'=8,'agents_1'=4,'agents_2'=2,'group'=4] {'agents_0','agen..., dimensions={0} | all-to-all | bytes 262144 | tf_op jit(solution)/shard_map/all_to_all | solution.py:137
  (203 shorter events, 91.2 us)
Async XLA Ops:
  2.4 11.5 %collective-permute-start.4 = (f32[41,128]{1,0:T(8,128)S(1)}, f32[41,128]{1,0:T(8,128)S(1)}, u32[]{:S(2)}, u32[]{:S(2)}) collective-permute-start(f32[41,128]{1,0:T(8,128)S(1)} %pad_maximum_fusion), channel_id=1, source_target_pairs={{4,0},{0,4},{36,32},{32,36},{68,64},{64,68},{100,96},{96,100},{132... | collective-permute-start | bytes 62984 | tf_op jit(solution)/shard_map/ppermute | solution.py:32
  5.7 10.1 %collective-permute-start.5 = (f32[41,128]{1,0:T(8,128)S(1)}, f32[41,128]{1,0:T(8,128)S(1)}, u32[]{:S(2)}, u32[]{:S(2)}) collective-permute-start(f32[41,128]{1,0:T(8,128)S(1)} %pad_maximum_fusion), channel_id=1, source_target_pairs={{32,0},{36,4},{0,32},{4,36},{96,64},{100,68},{64,96},{68,100},{160... | collective-permute-start | bytes 62984 | tf_op jit(solution)/shard_map/ppermute | solution.py:32
  5.7 11.5 %collective-permute-start.6 = (f32[41,128]{1,0:T(8,128)S(1)}, f32[41,128]{1,0:T(8,128)S(1)}, u32[]{:S(2)}, u32[]{:S(2)}) collective-permute-start(f32[41,128]{1,0:T(8,128)S(1)} %pad_maximum_fusion), channel_id=1, source_target_pairs={{36,0},{32,4},{4,32},{0,36},{100,64},{96,68},{68,96},{64,100},{164... | collective-permute-start | bytes 62984 | tf_op jit(solution)/shard_map/ppermute | solution.py:32
  7.5 18.2 %collective-permute-start = (f32[1,40,256]{2,1,0:T(8,128)}, f32[1,40,256]{2,1,0:T(8,128)S(1)}, u32[]{:S(2)}, u32[]{:S(2)}) collective-permute-start(f32[1,40,256]{2,1,0:T(8,128)} %param.14), channel_id=1, source_target_pairs={{0,8},{4,12},{8,16},{12,20},{16,24},{20,28},{24,32},{28,36},{32,40... | collective-permute-start | bytes 122888 | tf_op jit(solution)/shard_map/ppermute | solution.py:24
  8.9 18.0 %collective-permute-start.1 = (f32[1,40,256]{2,1,0:T(8,128)}, f32[1,40,256]{2,1,0:T(8,128)S(1)}, u32[]{:S(2)}, u32[]{:S(2)}) collective-permute-start(f32[1,40,256]{2,1,0:T(8,128)} %param.14), channel_id=1, source_target_pairs={{0,4},{4,8},{8,12},{12,16},{16,20},{20,24},{24,28},{28,32},{32,36}... | collective-permute-start | bytes 122888 | tf_op jit(solution)/shard_map/ppermute | solution.py:24
  13.9 14.7 %collective-permute-start.2 = (f32[1,40,256]{2,1,0:T(8,128)}, f32[1,40,256]{2,1,0:T(8,128)S(1)}, u32[]{:S(2)}, u32[]{:S(2)}) collective-permute-start(f32[1,40,256]{2,1,0:T(8,128)} %param.14), channel_id=1, source_target_pairs={{4,0},{8,4},{12,8},{16,12},{20,16},{24,20},{28,24},{32,28},{36,32}... | collective-permute-start | bytes 122888 | tf_op jit(solution)/shard_map/ppermute | solution.py:24
  15.9 12.8 %collective-permute-start.3 = (f32[1,40,256]{2,1,0:T(8,128)}, f32[1,40,256]{2,1,0:T(8,128)S(1)}, u32[]{:S(2)}, u32[]{:S(2)}) collective-permute-start(f32[1,40,256]{2,1,0:T(8,128)} %param.14), channel_id=1, source_target_pairs={{8,0},{12,4},{16,8},{20,12},{24,16},{28,20},{32,24},{36,28},{40,32... | collective-permute-start | bytes 122888 | tf_op jit(solution)/shard_map/ppermute | solution.py:24
  17.2 17.2 %collective-permute-start.7 = (f32[41,128]{1,0:T(8,128)S(1)}, f32[41,128]{1,0:T(8,128)S(1)}, u32[]{:S(2)}, u32[]{:S(2)}) collective-permute-start(f32[41,128]{1,0:T(8,128)S(1)} %add_add_fusion.3), channel_id=1, source_target_pairs={{224,0},{64,32},{32,64},{128,96},{96,128},{192,160},{160,192},{0,2... | collective-permute-start | bytes 62984 | tf_op jit(solution)/shard_map/ppermute | solution.py:32
  25.7 8.7 %collective-permute-start.8 = (f32[41,128]{1,0:T(8,128)S(1)}, f32[41,128]{1,0:T(8,128)S(1)}, u32[]{:S(2)}, u32[]{:S(2)}) collective-permute-start(f32[41,128]{1,0:T(8,128)S(1)} %add_add_fusion.3), channel_id=1, source_target_pairs={{64,0},{224,32},{128,64},{32,96},{192,128},{96,160},{0,192},{160,2... | collective-permute-start | bytes 62984 | tf_op jit(solution)/shard_map/ppermute | solution.py:32
  26.9 7.6 %collective-permute-start.9 = (f32[41,128]{1,0:T(8,128)S(1)}, f32[41,128]{1,0:T(8,128)S(1)}, u32[]{:S(2)}, u32[]{:S(2)}) collective-permute-start(f32[41,128]{1,0:T(8,128)S(1)} %add_add_fusion.3), channel_id=1, source_target_pairs={{160,0},{128,32},{224,64},{192,96},{32,128},{0,160},{96,192},{64,2... | collective-permute-start | bytes 62984 | tf_op jit(solution)/shard_map/ppermute | solution.py:32
  48.2 13.6 %collective-permute-start.16 = (f32[1,40,256]{2,1,0:T(8,128)S(1)}, f32[1,40,256]{2,1,0:T(8,128)S(1)}, u32[]{:S(2)}, u32[]{:S(2)}) collective-permute-start(f32[1,40,256]{2,1,0:T(8,128)S(1)} %bitcast_add_fusion.7), channel_id=1, source_target_pairs={{0,8},{4,12},{8,16},{12,20},{16,24},{20,28},{24,32},{28,36},{32,40... | collective-permute-start | bytes 122888 | tf_op jit(solution)/shard_map/ppermute | solution.py:24
  50.7 11.2 %collective-permute-start.17 = (f32[1,40,256]{2,1,0:T(8,128)S(1)}, f32[1,40,256]{2,1,0:T(8,128)S(1)}, u32[]{:S(2)}, u32[]{:S(2)}) collective-permute-start(f32[1,40,256]{2,1,0:T(8,128)S(1)} %bitcast_add_fusion.7), channel_id=1, source_target_pairs={{0,4},{4,8},{8,12},{12,16},{16,20},{20,24},{24,28},{28,32},{32,36}... | collective-permute-start | bytes 122888 | tf_op jit(solution)/shard_map/ppermute | solution.py:24
  58.4 5.3 %collective-permute-start.18 = (f32[1,40,256]{2,1,0:T(8,128)S(1)}, f32[1,40,256]{2,1,0:T(8,128)S(1)}, u32[]{:S(2)}, u32[]{:S(2)}) collective-permute-start(f32[1,40,256]{2,1,0:T(8,128)S(1)} %bitcast_add_fusion.7), channel_id=1, source_target_pairs={{4,0},{8,4},{12,8},{16,12},{20,16},{24,20},{28,24},{32,28},{36,32}... | collective-permute-start | bytes 122888 | tf_op jit(solution)/shard_map/ppermute | solution.py:24
  76.0 6.9 %collective-permute-start.20 = (f32[41,128]{1,0:T(8,128)S(1)}, f32[41,128]{1,0:T(8,128)S(1)}, u32[]{:S(2)}, u32[]{:S(2)}) collective-permute-start(f32[41,128]{1,0:T(8,128)S(1)} %concatenate.24), channel_id=1, source_target_pairs={{4,0},{0,4},{36,32},{32,36},{68,64},{64,68},{100,96},{96,100},{132... | collective-permute-start | bytes 62984 | tf_op jit(solution)/shard_map/ppermute | solution.py:32
  77.4 6.5 %collective-permute-start.21 = (f32[41,128]{1,0:T(8,128)S(1)}, f32[41,128]{1,0:T(8,128)S(1)}, u32[]{:S(2)}, u32[]{:S(2)}) collective-permute-start(f32[41,128]{1,0:T(8,128)S(1)} %concatenate.24), channel_id=1, source_target_pairs={{32,0},{36,4},{0,32},{4,36},{96,64},{100,68},{64,96},{68,100},{160... | collective-permute-start | bytes 62984 | tf_op jit(solution)/shard_map/ppermute | solution.py:32
  86.9 5.8 %collective-permute-start.23 = (f32[41,128]{1,0:T(8,128)S(1)}, f32[41,128]{1,0:T(8,128)S(1)}, u32[]{:S(2)}, u32[]{:S(2)}) collective-permute-start(f32[41,128]{1,0:T(8,128)S(1)} %maximum_select_fusion.7), channel_id=1, source_target_pairs={{224,0},{64,32},{32,64},{128,96},{96,128},{192,160},{160,192},{0,2... | collective-permute-start | bytes 62984 | tf_op jit(solution)/shard_map/ppermute | solution.py:32
  92.8 5.7 %collective-permute-start.25 = (f32[41,128]{1,0:T(8,128)S(1)}, f32[41,128]{1,0:T(8,128)S(1)}, u32[]{:S(2)}, u32[]{:S(2)}) collective-permute-start(f32[41,128]{1,0:T(8,128)S(1)} %maximum_select_fusion.7), channel_id=1, source_target_pairs={{160,0},{128,32},{224,64},{192,96},{32,128},{0,160},{96,192},{64,2... | collective-permute-start | bytes 62984 | tf_op jit(solution)/shard_map/ppermute | solution.py:32
  111.9 13.7 %collective-permute-start.32 = (f32[1,40,256]{2,1,0:T(8,128)S(1)}, f32[1,40,256]{2,1,0:T(8,128)S(1)}, u32[]{:S(2)}, u32[]{:S(2)}) collective-permute-start(f32[1,40,256]{2,1,0:T(8,128)S(1)} %bitcast_add_fusion.5), channel_id=1, source_target_pairs={{0,8},{4,12},{8,16},{12,20},{16,24},{20,28},{24,32},{28,36},{32,40... | collective-permute-start | bytes 122888 | tf_op jit(solution)/shard_map/ppermute | solution.py:24
  114.1 11.5 %collective-permute-start.33 = (f32[1,40,256]{2,1,0:T(8,128)S(1)}, f32[1,40,256]{2,1,0:T(8,128)S(1)}, u32[]{:S(2)}, u32[]{:S(2)}) collective-permute-start(f32[1,40,256]{2,1,0:T(8,128)S(1)} %bitcast_add_fusion.5), channel_id=1, source_target_pairs={{0,4},{4,8},{8,12},{12,16},{16,20},{20,24},{24,28},{28,32},{32,36}... | collective-permute-start | bytes 122888 | tf_op jit(solution)/shard_map/ppermute | solution.py:24
  122.2 5.3 %collective-permute-start.34 = (f32[1,40,256]{2,1,0:T(8,128)S(1)}, f32[1,40,256]{2,1,0:T(8,128)S(1)}, u32[]{:S(2)}, u32[]{:S(2)}) collective-permute-start(f32[1,40,256]{2,1,0:T(8,128)S(1)} %bitcast_add_fusion.5), channel_id=1, source_target_pairs={{4,0},{8,4},{12,8},{16,12},{20,16},{24,20},{28,24},{32,28},{36,32}... | collective-permute-start | bytes 122888 | tf_op jit(solution)/shard_map/ppermute | solution.py:24
  155.7 5.8 %collective-permute-start.41 = (f32[41,128]{1,0:T(8,128)S(1)}, f32[41,128]{1,0:T(8,128)S(1)}, u32[]{:S(2)}, u32[]{:S(2)}) collective-permute-start(f32[41,128]{1,0:T(8,128)S(1)} %maximum_select_fusion.3), channel_id=1, source_target_pairs={{160,0},{128,32},{224,64},{192,96},{32,128},{0,160},{96,192},{64,2... | collective-permute-start | bytes 62984 | tf_op jit(solution)/shard_map/ppermute | solution.py:32
  176.8 13.8 %collective-permute-start.48 = (f32[1,40,256]{2,1,0:T(8,128)S(1)}, f32[1,40,256]{2,1,0:T(8,128)S(1)}, u32[]{:S(2)}, u32[]{:S(2)}) collective-permute-start(f32[1,40,256]{2,1,0:T(8,128)S(1)} %bitcast_add_fusion.3), channel_id=1, source_target_pairs={{0,8},{4,12},{8,16},{12,20},{16,24},{20,28},{24,32},{28,36},{32,40... | collective-permute-start | bytes 122888 | tf_op jit(solution)/shard_map/ppermute | solution.py:24
  178.2 12.5 %collective-permute-start.49 = (f32[1,40,256]{2,1,0:T(8,128)S(1)}, f32[1,40,256]{2,1,0:T(8,128)S(1)}, u32[]{:S(2)}, u32[]{:S(2)}) collective-permute-start(f32[1,40,256]{2,1,0:T(8,128)S(1)} %bitcast_add_fusion.3), channel_id=1, source_target_pairs={{0,4},{4,8},{8,12},{12,16},{16,20},{20,24},{24,28},{28,32},{32,36}... | collective-permute-start | bytes 122888 | tf_op jit(solution)/shard_map/ppermute | solution.py:24
  187.4 5.3 %collective-permute-start.50 = (f32[1,40,256]{2,1,0:T(8,128)S(1)}, f32[1,40,256]{2,1,0:T(8,128)S(1)}, u32[]{:S(2)}, u32[]{:S(2)}) collective-permute-start(f32[1,40,256]{2,1,0:T(8,128)S(1)} %bitcast_add_fusion.3), channel_id=1, source_target_pairs={{4,0},{8,4},{12,8},{16,12},{20,16},{24,20},{28,24},{32,28},{36,32}... | collective-permute-start | bytes 122888 | tf_op jit(solution)/shard_map/ppermute | solution.py:24
  (40 other events, 360.8 us)

commit v2 on v1

v2 whole, which is shorter than its diff:
```python
import functools
import itertools

import jax
import jax.numpy as jnp
from jax import lax
from jax.experimental import pallas as pl
from jax.experimental.pallas import tpu as pltpu
from jax.sharding import Mesh
from jax.sharding import PartitionSpec as P

SPAN = 2
NPLAT = 128
ITERS = 3
LANES = 128
AGENTS = ("agents_0", "agents_1", "agents_2")
AGENTS_GROUP = ("agents_0", "agents_1", "agents_2", "group")


RHO = 0.5
KAPPA = 0.5


def shifted(value, axis, steps):
    count = lax.axis_size(axis)
    first, last = (max(0, -steps), min(count, count - steps))
    return lax.ppermute(value, axis, [(source, source + steps) for source in range(first, last)])


def exchanged(value, axes, sources):
    sizes = [lax.axis_size(axis) for axis in axes]
    places = list(itertools.product(*[range(size) for size in sizes]))
    at = {place: k for k, place in enumerate(places)}
    return [value] + [
        lax.ppermute(value, axes, [(at[source(*place)], at[place]) for place in places])
        for source in sources
    ]


PAIRS = [lambda z, c: (z, 1 - c), lambda z, c: (z ^ 1, c), lambda z, c: (z ^ 1, 1 - c)]
OTHERS = [
    lambda z: ((z - 1 + 2 * (z % 2)) % 8,),
    lambda z: ((z + 2 - 4 * (z % 2)) % 8,),
    lambda z: (z ^ 5,),
]


def gathered(value, combine):
    value = combine(exchanged(value, ("agents_0", "agents_2"), PAIRS))
    value = combine(exchanged(value, ("agents_0",), OTHERS))
    axes = ("agents_1", "group")
    every = jnp.broadcast_to(value[None], (lax.axis_size(axes), *value.shape))
    return lax.all_to_all(every, axes, 0, 0, tiled=True)


def neighbours(field):
    count = lax.axis_size(AGENTS)
    near = [(k, k + 1 if k % 2 else k - 1) for k in range(count)]
    return (
        field,
        lax.ppermute(field, "agents_2", [(0, 1), (1, 0)]),
        lax.ppermute(field, AGENTS, [(a, b) for a, b in near if 0 <= b < count]),
        shifted(field, AGENTS, 2),
        shifted(field, AGENTS, -2),
    )


def gap_kernel(column, offsets, own, *rest):
    fields, (gap, total, peak) = ((own, *rest[:4]), rest[4:])
    degree, length, block = offsets.shape
    wide = (length, LANES)
    largest = jnp.zeros(wide, jnp.float32)
    for first in range(0, block, LANES):
        here = own[:, first : first + LANES]
        added = jnp.zeros(wide, jnp.float32)
        for k in range(degree):
            index = jnp.broadcast_to(column[k : k + 1, first : first + LANES], wide)
            lane, tile = (index & (LANES - 1), index >> 7)
            near = jnp.zeros(wide, jnp.float32)
            for at in range(len(fields) * block // LANES):
                field = fields[at * LANES // block]
                start = at * LANES % block
                taken = jnp.take_along_axis(
                    field[:, start : start + LANES], lane, axis=1, mode="promise_in_bounds"
                )
                near = jnp.where(tile == at, taken, near)
            value = jnp.where(
                index >= 0, here - near - offsets[k, :, first : first + LANES], 0.0
            )
            gap[k, :, first : first + LANES] = value
            added += value
            largest = jnp.maximum(largest, jnp.abs(value))
        total[:, first : first + LANES] = added
    peak[...] = jnp.broadcast_to(jnp.max(largest), peak.shape)


def gaps(column, offsets, fields, rows):
    degree, length, block = offsets.shape
    return pl.pallas_call(
        gap_kernel,
        out_shape=(
            jax.ShapeDtypeStruct((degree, length, block), jnp.float32),
            jax.ShapeDtypeStruct((length, block), jnp.float32),
            jax.ShapeDtypeStruct((rows, LANES), jnp.float32),
        ),
        compiler_params=pltpu.CompilerParams(vmem_limit_bytes=16 * 1024 * 1024),
        name="gaps",
    )(column, offsets, *fields)


def solve_kernel(first, *refs):
    parts, counts, platoon, q_lin, inverse, predict, free, lam, total, traj, alive = refs[:11]
    plan_out, traj_out, sums_out, scale_out, lam_out = refs[11:]
    length, block = free.shape
    whole = parts[0]
    used = counts[...] > 0.5
    if first:
        for k in range(1, parts.shape[0]):
            whole += parts[k]
        whole = whole[:length]
        scale = jnp.zeros((1, 1), jnp.float32)
    else:
        most = whole
        for k in range(1, parts.shape[0]):
            whole += parts[k]
            most = jnp.maximum(most, parts[k])
        peak = jnp.max(jnp.where(used, 0.0, most), keepdims=True)
        scale = 1.0 / (1.0 + peak)
    means = jnp.where(used, whole, 0.0) / jnp.maximum(counts[...], 1.0)
    onehot = (
        lax.broadcasted_iota(jnp.int32, (NPLAT, block), 0) == platoon[...]
    ).astype(jnp.float32)
    attract = jnp.dot(
        means, onehot, precision=lax.Precision.HIGHEST, preferred_element_type=jnp.float32
    )
    lam_new = lam[...] + scale * total[...] if not first else lam[...]
    coupling = lam_new - RHO * (alive[...] * traj[...] - total[...]) - KAPPA * attract
    rhs = q_lin[...]
    for t in range(length):
        rhs += predict[t].astype(jnp.float32) * coupling[t : t + 1]
    plan = jnp.zeros(rhs.shape, jnp.float32)
    for i in range(rhs.shape[0]):
        plan -= inverse[i].astype(jnp.float32) * rhs[i : i + 1]
    plan_out[...] = plan
    for t in range(length):
        traj_out[t : t + 1] = free[t : t + 1] + jnp.sum(
            predict[t].astype(jnp.float32) * plan, axis=0, keepdims=True
        )
    sums_out[...] = lax.dot_general(
        traj_out[...],
        onehot,
        (((1,), (1,)), ((), ())),
        precision=lax.Precision.HIGHEST,
        preferred_element_type=jnp.float32,
    )
    scale_out[...] = jnp.broadcast_to(scale, scale_out.shape)
    lam_out[...] = lam_new


def solved(first, *args):
    length, block = args[6].shape
    qp = args[3].shape[0]
    return pl.pallas_call(
        functools.partial(solve_kernel, first),
        out_shape=(
            jax.ShapeDtypeStruct((qp, block), jnp.float32),
            jax.ShapeDtypeStruct((length, block), jnp.float32),
            jax.ShapeDtypeStruct((length, NPLAT), jnp.float32),
            jax.ShapeDtypeStruct((8, LANES), jnp.float32),
            jax.ShapeDtypeStruct((length, block), jnp.float32),
        ),
        compiler_params=pltpu.CompilerParams(vmem_limit_bytes=16 * 1024 * 1024),
        name="solve",
    )(*args)


def added(pieces):
    return sum(pieces[1:], pieces[0])


def local(q_lin, inverse, predict, free_traj, offsets, multipliers, nbr_owner, nbr_slot, platoon):
    block = q_lin.shape[2]
    traj_len = free_traj.shape[1]
    q_lin, inverse, predict, free_traj = (q_lin[0], inverse[0], predict[0], free_traj[0])
    offsets, multipliers, owner, slot = (offsets[0], multipliers[0], nbr_owner[0], nbr_slot[0])
    live = slot >= 0
    onehot = (platoon == jnp.arange(NPLAT, dtype=jnp.int32)[:, None]).astype(jnp.float32)
    mine = lax.axis_index(AGENTS)
    away = owner - mine
    beside = jnp.where((away > 0) == (mine % 2 == 0), 1, 2)
    place = jnp.where(away == 0, 0, jnp.where(abs(away) == 1, beside, jnp.where(away < 0, 3, 4)))
    column = jnp.where(live, place * block + slot, -1)
    alive = jnp.sum(live.astype(jnp.float32), axis=0, keepdims=True)
    lam = jnp.sum(jnp.where(live[:, None, :], multipliers, 0.0), axis=0)

    sums = jnp.einsum("ta,pa->tp", free_traj, onehot, precision=lax.Precision.HIGHEST)
    counts = jnp.sum(onehot, axis=1)[None]
    packed = jnp.concatenate([sums, counts, jnp.zeros((7, NPLAT), jnp.float32)])
    parts = gathered(packed, added)
    parts = parts.reshape(-1, *packed.shape)
    counts = jnp.sum(parts[:, traj_len], axis=0, keepdims=True)
    unused = counts < 0.5

    def joined(pieces):
        return jnp.where(unused, functools.reduce(jnp.maximum, pieces), added(pieces))

    traj = free_traj
    _, total, _ = gaps(column, offsets, neighbours(traj), 8)
    new_multipliers = multipliers
    for step in range(ITERS):
        plan, traj, sums, scale, lam = solved(
            step == 0, parts, counts, platoon, q_lin, inverse, predict, free_traj, lam, total, traj, alive
        )
        if step > 0:
            new_multipliers = new_multipliers + scale[0, 0] * gap
        more = step + 1 < ITERS
        count = lax.axis_size(AGENTS_GROUP)
        gap, total, peak = gaps(column, offsets, neighbours(traj), 8 if more else count)
        if more:
            packed = jnp.where(unused, peak[:1], sums)
            parts = gathered(packed, joined).reshape(-1, *packed.shape)
        else:
            peak = jnp.max(lax.all_to_all(peak, AGENTS_GROUP, 0, 0, tiled=True))
            new_multipliers = new_multipliers + gap / (1.0 + peak)
    return (plan[None], new_multipliers[None])


def solution(mesh):
    finer = Mesh(
        mesh.devices.reshape(8, 4, 2, mesh.shape["group"]),
        ("agents_0", "agents_1", "agents_2", "group"),
    )
    placed = (
        P("group", None, AGENTS),
        P("group", None, None, AGENTS),
        P("group", None, None, AGENTS),
        P("group", None, AGENTS),
        P("group", None, None, AGENTS),
        P("group", None, None, AGENTS),
        P("group", None, AGENTS),
        P("group", None, AGENTS),
        P("group", AGENTS),
    )
    return jax.shard_map(
        local,
        mesh=finer,
        in_specs=placed,
        out_specs=(P("group", None, AGENTS), P("group", None, None, AGENTS)),
        check_vma=False,
    )
```

time: 231 us -> 175 us (0.76)
  local copies, waits for them, and re-layouts: 34.1 us -> 2.73 us
  waiting for transfers between devices: 45.9 us -> 31 us
  other arithmetic: 16.6 us -> 3.39 us
  Pallas kernels: 0 us -> 10.3 us
  blocking collectives: 26.5 us -> 22.9 us
    ppermute x36 -> x18, waiting for transfers between devices: 36.2 us -> 7.6 us  [exchanged(): lax.ppermute(value, axes, [(at[source(*place)], at[place]) for place in p...]
    ppermute x16 -> x8, starting transfers between devices: 48.8 us -> 21.1 us  [shifted(): lax.ppermute(value, axis, [(source, source + steps) for source in range(f...]
    gather x4 -> x0, local copies, waits for them, and re-layouts: 26.1 us -> none  [lookup(): jnp.take(joined[0], column, axis=1)]
    all_to_all x0 -> x2, starting transfers between devices: none -> 21 us  [the longest x1 12.3 us: local(): peak = jnp.max(lax.all_to_all(peak, AGENTS_GROUP, 0, 0, tiled=True))]
    ppermute x0 -> x8, starting transfers between devices: none -> 20.3 us  [the longest x4 19.9 us: neighbours(): lax.ppermute(field, AGENTS, [(a, b) for a, b in near if 0 <= b < count])]
    all_to_all x0 -> x2, waiting for transfers between devices: none -> 18.8 us  [the longest x1 11.6 us: local(): peak = jnp.max(lax.all_to_all(peak, AGENTS_GROUP, 0, 0, tiled=True))]
    ppermute x36 -> x18, starting transfers between devices: 53.1 us -> 38.4 us  [exchanged(): lax.ppermute(value, axes, [(at[source(*place)], at[place]) for place in p...]
    pallas_call x0 -> x7, Pallas kernels: none -> 10.3 us  [the longest x4 5.66 us: gaps(): pl.pallas_call(gap_kernel, out_shape=(jax.ShapeDtypeStruct((degree, lengt...]
  transfers between devices with their start and end apart: 52 -> 36, of which waited for: 28 -> 10; matrix products, arithmetic and copies ran while one was open for 5% -> 1% of each run, Pallas kernels for 0% -> 1%
where the time goes in v2:
time: 175 us; the launch traced here: 174 us
  starting transfers between devices  101 us (58%)
  waiting for transfers between devices  31 us (18%)
  blocking collectives  22.9 us (13%)
  Pallas kernels  10.3 us (6%)
  other arithmetic  3.39 us (2%)
  local copies, waits for them, and re-layouts  2.73 us (2%)
  between operations  1.79 us (1%)
    ppermute x18, starting transfers between devices, exchanged(): lax.ppermute(value, axes, [(at[source(*place)], at[place]) for place in p...  38.4 us
    all_to_all x2, blocking collectives, gathered(): return lax.all_to_all(every, axes, 0, 0, tiled=True)  22.9 us
    ppermute x8, starting transfers between devices, shifted(): lax.ppermute(value, axis, [(source, source + steps) for source in range(f...  21.1 us
    ppermute x4, starting transfers between devices, neighbours(): lax.ppermute(field, AGENTS, [(a, b) for a, b in near if 0 <= b < count])  19.9 us
    all_to_all x1, starting transfers between devices, local(): peak = jnp.max(lax.all_to_all(peak, AGENTS_GROUP, 0, 0, tiled=True))  12.3 us
    all_to_all x1, waiting for transfers between devices, local(): peak = jnp.max(lax.all_to_all(peak, AGENTS_GROUP, 0, 0, tiled=True))  11.6 us
    all_to_all x1, starting transfers between devices, gathered(): return lax.all_to_all(every, axes, 0, 0, tiled=True)  8.7 us
    ppermute x18, waiting for transfers between devices, exchanged(): lax.ppermute(value, axes, [(at[source(*place)], at[place]) for place in p...  7.6 us
  transfers between devices with their start and end apart: 36, of which 10 were waited for; matrix products, arithmetic and copies ran while one was open for 1% of the time, Pallas kernels for 1%

profile of v2, /device:TPU:1, one launch (start us, length us, event | category | flops | bytes accessed | tf_op | source)
XLA Modules:
  0.0 174.0 jit_solution(4804383657607218529)
XLA Ops:
  2.6 2.5 %collective-permute-start.1 = (f32[48,128]{1,0:T(8,128)S(1)}, f32[48,128]{1,0:T(8,128)S(1)}, u32[]{:S(2)}, u32[]{:S(2)}) collective-permute-start(f32[48,128]{1,0:T(8,128)S(1)} %maximum_maximum_fusion), channel_id=1, source_target_pairs={{32,0},{36,4},{0,32},{4,36},{96,64},{100,68},{64,96},{68,100},{160... | collective-permute-start | bytes 73736 | tf_op jit(solution)/shard_map/ppermute | solution.py:35
  5.1 2.4 %collective-permute-start.2 = (f32[48,128]{1,0:T(8,128)S(1)}, f32[48,128]{1,0:T(8,128)S(1)}, u32[]{:S(2)}, u32[]{:S(2)}) collective-permute-start(f32[48,128]{1,0:T(8,128)S(1)} %maximum_maximum_fusion), channel_id=1, source_target_pairs={{36,0},{32,4},{4,32},{0,36},{100,64},{96,68},{68,96},{64,100},{164... | collective-permute-start | bytes 73736 | tf_op jit(solution)/shard_map/ppermute | solution.py:35
  9.3 5.2 %collective-permute-start.5 = (f32[48,128]{1,0:T(8,128)S(1)}, f32[48,128]{1,0:T(8,128)S(1)}, u32[]{:S(2)}, u32[]{:S(2)}) collective-permute-start(f32[48,128]{1,0:T(8,128)S(1)} %add_add_fusion.1), channel_id=1, source_target_pairs={{160,0},{128,32},{224,64},{192,96},{32,128},{0,160},{96,192},{64,2... | collective-permute-start | bytes 73736 | tf_op jit(solution)/shard_map/ppermute | solution.py:35
  14.5 3.1 %collective-permute-start.3 = (f32[48,128]{1,0:T(8,128)S(1)}, f32[48,128]{1,0:T(8,128)S(1)}, u32[]{:S(2)}, u32[]{:S(2)}) collective-permute-start(f32[48,128]{1,0:T(8,128)S(1)} %add_add_fusion.1), channel_id=1, source_target_pairs={{224,0},{64,32},{32,64},{128,96},{96,128},{192,160},{160,192},{0,2... | collective-permute-start | bytes 73736 | tf_op jit(solution)/shard_map/ppermute | solution.py:35
  18.9 4.0 %collective-permute-start.8 = (f32[40,256]{1,0:T(8,128)S(1)}, f32[40,256]{1,0:T(8,128)S(1)}, u32[]{:S(2)}, u32[]{:S(2)}) collective-permute-start(f32[40,256]{1,0:T(8,128)S(1)} %bitcast.52), channel_id=1, source_target_pairs={{0,8},{4,12},{8,16},{12,20},{16,24},{20,28},{24,32},{28,36},{32,40... | collective-permute-start | bytes 122888 | tf_op jit(solution)/shard_map/ppermute | solution.py:27
  22.9 5.0 %collective-permute-start.7 = (f32[40,256]{1,0:T(8,128)S(1)}, f32[40,256]{1,0:T(8,128)S(1)}, u32[]{:S(2)}, u32[]{:S(2)}) collective-permute-start(f32[40,256]{1,0:T(8,128)S(1)} %bitcast.53), channel_id=1, source_target_pairs={{4,8},{8,4},{12,16},{16,12},{20,24},{24,20},{28,32},{32,28},{36,40... | collective-permute-start | bytes 122888 | tf_op jit(solution)/shard_map/ppermute | solution.py:62
  28.9 8.7 %all-to-all-start = ((f32[16,48,128]{2,1,0:T(8,128)}), f32[16,48,128]{2,1,0:T(8,128)S(1)}, u32[]{:S(2)}, u32[]{:S(2)}) async-start(f32[16,48,128]{2,1,0:T(8,128)} %broadcast_in_dim.111), calls=%async_computation | async-start | bytes 786432 | tf_op jit(solution)/shard_map/all_to_all | solution.py:53
  39.5 7.2 %all-to-all-done.refs_0_ = f32[16,48,128]{2,1,0:T(8,128)S(1)} async-done(((f32[16,48,128]{2,1,0:T(8,128)}), f32[16,48,128]{2,1,0:T(8,128)S(1)}, u32[]{:S(2)}, u32[]{:S(2)}) %all-to-all-start) | async-done | bytes 393248 | tf_op jit(solution)/shard_map/all_to_all | solution.py:53
  49.5 4.0 %collective-permute-start.12 = (f32[40,256]{1,0:T(8,128)S(1)}, f32[40,256]{1,0:T(8,128)S(1)}, u32[]{:S(2)}, u32[]{:S(2)}) collective-permute-start(f32[40,256]{1,0:T(8,128)S(1)} %get-tuple-element.22.own.refs_9_), channel_id=1, source_target_pairs={{0,8},{4,12},{8,16},{12,20},{16,24},{20,28},{24,32},{28,36},{32,40... | collective-permute-start | bytes 122888 | tf_op jit(solution)/shard_map/ppermute | solution.py:27
  53.5 3.8 %collective-permute-start.11 = (f32[40,256]{1,0:T(8,128)S(1)}, f32[40,256]{1,0:T(8,128)S(1)}, u32[]{:S(2)}, u32[]{:S(2)}) collective-permute-start(f32[40,256]{1,0:T(8,128)S(1)} %get-tuple-element.22.own.refs_9_), channel_id=1, source_target_pairs={{4,8},{8,4},{12,16},{16,12},{20,24},{24,20},{28,32},{32,28},{36,40... | collective-permute-start | bytes 122888 | tf_op jit(solution)/shard_map/ppermute | solution.py:62
  62.2 2.7 %collective-permute-start.16 = (f32[40,128]{1,0:T(8,128)S(1)}, f32[40,128]{1,0:T(8,128)S(1)}, u32[]{:S(2)}, u32[]{:S(2)}) collective-permute-start(f32[40,128]{1,0:T(8,128)S(1)} %broadcast_select_fusion.1), channel_id=1, source_target_pairs={{36,0},{32,4},{4,32},{0,36},{100,64},{96,68},{68,96},{64,100},{164... | collective-permute-start | bytes 61448 | tf_op jit(solution)/shard_map/ppermute | solution.py:35
  66.5 5.4 %collective-permute-start.19 = (f32[40,128]{1,0:T(8,128)S(1)}, f32[40,128]{1,0:T(8,128)S(1)}, u32[]{:S(2)}, u32[]{:S(2)}) collective-permute-start(f32[40,128]{1,0:T(8,128)S(1)} %add_select_fusion.3), channel_id=1, source_target_pairs={{160,0},{128,32},{224,64},{192,96},{32,128},{0,160},{96,192},{64,2... | collective-permute-start | bytes 61448 | tf_op jit(solution)/shard_map/ppermute | solution.py:35
  73.1 2.9 %collective-permute-start.17 = (f32[40,128]{1,0:T(8,128)S(1)}, f32[40,128]{1,0:T(8,128)S(1)}, u32[]{:S(2)}, u32[]{:S(2)}) collective-permute-start(f32[40,128]{1,0:T(8,128)S(1)} %add_select_fusion.3), channel_id=1, source_target_pairs={{224,0},{64,32},{32,64},{128,96},{96,128},{192,160},{160,192},{0,2... | collective-permute-start | bytes 61448 | tf_op jit(solution)/shard_map/ppermute | solution.py:35
  77.5 11.6 %all_to_all.24.refs_0_ = f32[16,40,128]{2,1,0:T(8,128)S(1)} all-to-all(f32[16,40,128]{2,1,0:T(8,128)S(1)} %broadcast_in_dim.122), channel_id=1, replica_groups=mesh['agents_0'=8,'agents_1'=4,'agents_2'=2,'group'=4] {'agents_1','group'}, dimensions={0} | all-to-all | bytes 655360 | tf_op jit(solution)/shard_map/all_to_all | solution.py:53
  91.8 4.0 %collective-permute-start.22 = (f32[40,256]{1,0:T(8,128)S(1)}, f32[40,256]{1,0:T(8,128)S(1)}, u32[]{:S(2)}, u32[]{:S(2)}) collective-permute-start(f32[40,256]{1,0:T(8,128)S(1)} %get-tuple-element.27.own.refs_9_), channel_id=1, source_target_pairs={{0,8},{4,12},{8,16},{12,20},{16,24},{20,28},{24,32},{28,36},{32,40... | collective-permute-start | bytes 122888 | tf_op jit(solution)/shard_map/ppermute | solution.py:27
  95.8 5.7 %collective-permute-start.21 = (f32[40,256]{1,0:T(8,128)S(1)}, f32[40,256]{1,0:T(8,128)S(1)}, u32[]{:S(2)}, u32[]{:S(2)}) collective-permute-start(f32[40,256]{1,0:T(8,128)S(1)} %get-tuple-element.27.own.refs_9_), channel_id=1, source_target_pairs={{4,8},{8,4},{12,16},{16,12},{20,24},{24,20},{28,32},{32,28},{36,40... | collective-permute-start | bytes 122888 | tf_op jit(solution)/shard_map/ppermute | solution.py:62
  104.4 4.4 %collective-permute-start.26 = (f32[40,128]{1,0:T(8,128)S(1)}, f32[40,128]{1,0:T(8,128)S(1)}, u32[]{:S(2)}, u32[]{:S(2)}) collective-permute-start(f32[40,128]{1,0:T(8,128)S(1)} %broadcast_select_fusion), channel_id=1, source_target_pairs={{36,0},{32,4},{4,32},{0,36},{100,64},{96,68},{68,96},{64,100},{164... | collective-permute-start | bytes 61448 | tf_op jit(solution)/shard_map/ppermute | solution.py:35
  110.5 2.2 %collective-permute-start.29 = (f32[40,128]{1,0:T(8,128)S(1)}, f32[40,128]{1,0:T(8,128)S(1)}, u32[]{:S(2)}, u32[]{:S(2)}) collective-permute-start(f32[40,128]{1,0:T(8,128)S(1)} %add_select_fusion.1), channel_id=1, source_target_pairs={{160,0},{128,32},{224,64},{192,96},{32,128},{0,160},{96,192},{64,2... | collective-permute-start | bytes 61448 | tf_op jit(solution)/shard_map/ppermute | solution.py:35
  113.8 2.7 %collective-permute-start.27 = (f32[40,128]{1,0:T(8,128)S(1)}, f32[40,128]{1,0:T(8,128)S(1)}, u32[]{:S(2)}, u32[]{:S(2)}) collective-permute-start(f32[40,128]{1,0:T(8,128)S(1)} %add_select_fusion.1), channel_id=1, source_target_pairs={{224,0},{64,32},{32,64},{128,96},{96,128},{192,160},{160,192},{0,2... | collective-permute-start | bytes 61448 | tf_op jit(solution)/shard_map/ppermute | solution.py:35
  118.2 11.4 %all_to_all.25.refs_0_ = f32[16,40,128]{2,1,0:T(8,128)S(1)} all-to-all(f32[16,40,128]{2,1,0:T(8,128)S(1)} %broadcast_in_dim.125), channel_id=1, replica_groups=mesh['agents_0'=8,'agents_1'=4,'agents_2'=2,'group'=4] {'agents_1','group'}, dimensions={0} | all-to-all | bytes 655360 | tf_op jit(solution)/shard_map/all_to_all | solution.py:53
  132.6 4.0 %collective-permute-start.32 = (f32[40,256]{1,0:T(8,128)S(1)}, f32[40,256]{1,0:T(8,128)S(1)}, u32[]{:S(2)}, u32[]{:S(2)}) collective-permute-start(f32[40,256]{1,0:T(8,128)S(1)} %get-tuple-element.37.own), channel_id=1, source_target_pairs={{0,8},{4,12},{8,16},{12,20},{16,24},{20,28},{24,32},{28,36},{32,40... | collective-permute-start | bytes 122888 | tf_op jit(solution)/shard_map/ppermute | solution.py:27
  136.6 5.4 %collective-permute-start.31 = (f32[40,256]{1,0:T(8,128)S(1)}, f32[40,256]{1,0:T(8,128)S(1)}, u32[]{:S(2)}, u32[]{:S(2)}) collective-permute-start(f32[40,256]{1,0:T(8,128)S(1)} %get-tuple-element.37.own), channel_id=1, source_target_pairs={{4,8},{8,4},{12,16},{16,12},{20,24},{24,20},{28,32},{32,28},{36,40... | collective-permute-start | bytes 122888 | tf_op jit(solution)/shard_map/ppermute | solution.py:62
  145.4 12.3 %all-to-all-start.3 = ((f32[256,1,128]{2,1,0:T(1,128)}), f32[256,1,128]{2,1,0:T(1,128)S(1)}, u32[]{:S(2)}, u32[]{:S(2)}) async-start(f32[256,1,128]{2,1,0:T(1,128)} %bitcast.19), calls=%async_computation.3 | async-start | bytes 262144 | tf_op jit(solution)/shard_map/all_to_all | solution.py:223
  158.8 11.6 %all-to-all-done.3 = f32[256,1,128]{2,1,0:T(1,128)S(1)} async-done(((f32[256,1,128]{2,1,0:T(1,128)}), f32[256,1,128]{2,1,0:T(1,128)S(1)}, u32[]{:S(2)}, u32[]{:S(2)}) %all-to-all-start.3) | async-done | bytes 131104 | tf_op jit(solution)/shard_map/all_to_all | solution.py:223
  (102 shorter events, 40.3 us)
Async XLA Ops:
  2.6 4.9 %collective-permute-start.1 = (f32[48,128]{1,0:T(8,128)S(1)}, f32[48,128]{1,0:T(8,128)S(1)}, u32[]{:S(2)}, u32[]{:S(2)}) collective-permute-start(f32[48,128]{1,0:T(8,128)S(1)} %maximum_maximum_fusion), channel_id=1, source_target_pairs={{32,0},{36,4},{0,32},{4,36},{96,64},{100,68},{64,96},{68,100},{160... | collective-permute-start | bytes 73736 | tf_op jit(solution)/shard_map/ppermute | solution.py:35
  9.3 13.6 %collective-permute-start.5 = (f32[48,128]{1,0:T(8,128)S(1)}, f32[48,128]{1,0:T(8,128)S(1)}, u32[]{:S(2)}, u32[]{:S(2)}) collective-permute-start(f32[48,128]{1,0:T(8,128)S(1)} %add_add_fusion.1), channel_id=1, source_target_pairs={{160,0},{128,32},{224,64},{192,96},{32,128},{0,160},{96,192},{64,2... | collective-permute-start | bytes 73736 | tf_op jit(solution)/shard_map/ppermute | solution.py:35
  14.5 13.4 %collective-permute-start.4 = (f32[48,128]{1,0:T(8,128)S(1)}, f32[48,128]{1,0:T(8,128)S(1)}, u32[]{:S(2)}, u32[]{:S(2)}) collective-permute-start(f32[48,128]{1,0:T(8,128)S(1)} %add_add_fusion.1), channel_id=1, source_target_pairs={{64,0},{224,32},{128,64},{32,96},{192,128},{96,160},{0,192},{160,2... | collective-permute-start | bytes 73736 | tf_op jit(solution)/shard_map/ppermute | solution.py:35
  14.5 13.5 %collective-permute-start.3 = (f32[48,128]{1,0:T(8,128)S(1)}, f32[48,128]{1,0:T(8,128)S(1)}, u32[]{:S(2)}, u32[]{:S(2)}) collective-permute-start(f32[48,128]{1,0:T(8,128)S(1)} %add_add_fusion.1), channel_id=1, source_target_pairs={{224,0},{64,32},{32,64},{128,96},{96,128},{192,160},{160,192},{0,2... | collective-permute-start | bytes 73736 | tf_op jit(solution)/shard_map/ppermute | solution.py:35
  17.6 20.1 %collective-permute-start.9 = (f32[40,256]{1,0:T(8,128)S(1)}, f32[40,256]{1,0:T(8,128)S(1)}, u32[]{:S(2)}, u32[]{:S(2)}) collective-permute-start(f32[40,256]{1,0:T(8,128)S(1)} %bitcast.51), channel_id=1, source_target_pairs={{8,0},{12,4},{16,8},{20,12},{24,16},{28,20},{32,24},{36,28},{40,32... | collective-permute-start | bytes 122888 | tf_op jit(solution)/shard_map/ppermute | solution.py:27
  18.9 18.8 %collective-permute-start.8 = (f32[40,256]{1,0:T(8,128)S(1)}, f32[40,256]{1,0:T(8,128)S(1)}, u32[]{:S(2)}, u32[]{:S(2)}) collective-permute-start(f32[40,256]{1,0:T(8,128)S(1)} %bitcast.52), channel_id=1, source_target_pairs={{0,8},{4,12},{8,16},{12,20},{16,24},{20,28},{24,32},{28,36},{32,40... | collective-permute-start | bytes 122888 | tf_op jit(solution)/shard_map/ppermute | solution.py:27
  22.9 14.8 %collective-permute-start.7 = (f32[40,256]{1,0:T(8,128)S(1)}, f32[40,256]{1,0:T(8,128)S(1)}, u32[]{:S(2)}, u32[]{:S(2)}) collective-permute-start(f32[40,256]{1,0:T(8,128)S(1)} %bitcast.53), channel_id=1, source_target_pairs={{4,8},{8,4},{12,16},{16,12},{20,24},{24,20},{28,32},{32,28},{36,40... | collective-permute-start | bytes 122888 | tf_op jit(solution)/shard_map/ppermute | solution.py:62
  27.9 9.8 %collective-permute-start.6 = (f32[40,256]{1,0:T(8,128)S(1)}, f32[40,256]{1,0:T(8,128)S(1)}, u32[]{:S(2)}, u32[]{:S(2)}) collective-permute-start(f32[40,256]{1,0:T(8,128)S(1)} %bitcast.54), channel_id=1, source_target_pairs={{0,4},{4,0},{1,5},{5,1},{2,6},{6,2},{3,7},{7,3},{8,12},{12,8},{9,1... | collective-permute-start | bytes 122888 | tf_op jit(solution)/shard_map/ppermute | solution.py:61
  28.9 17.8 %all-to-all-start = ((f32[16,48,128]{2,1,0:T(8,128)}), f32[16,48,128]{2,1,0:T(8,128)S(1)}, u32[]{:S(2)}, u32[]{:S(2)}) async-start(f32[16,48,128]{2,1,0:T(8,128)} %broadcast_in_dim.111), calls=%async_computation | async-start | bytes 786432 | tf_op jit(solution)/shard_map/all_to_all | solution.py:53
  48.2 9.2 %collective-permute-start.13 = (f32[40,256]{1,0:T(8,128)S(1)}, f32[40,256]{1,0:T(8,128)S(1)}, u32[]{:S(2)}, u32[]{:S(2)}) collective-permute-start(f32[40,256]{1,0:T(8,128)S(1)} %get-tuple-element.22.own.refs_9_), channel_id=1, source_target_pairs={{8,0},{12,4},{16,8},{20,12},{24,16},{28,20},{32,24},{36,28},{40,32... | collective-permute-start | bytes 122888 | tf_op jit(solution)/shard_map/ppermute | solution.py:27
  49.5 7.9 %collective-permute-start.12 = (f32[40,256]{1,0:T(8,128)S(1)}, f32[40,256]{1,0:T(8,128)S(1)}, u32[]{:S(2)}, u32[]{:S(2)}) collective-permute-start(f32[40,256]{1,0:T(8,128)S(1)} %get-tuple-element.22.own.refs_9_), channel_id=1, source_target_pairs={{0,8},{4,12},{8,16},{12,20},{16,24},{20,28},{24,32},{28,36},{32,40... | collective-permute-start | bytes 122888 | tf_op jit(solution)/shard_map/ppermute | solution.py:27
  53.5 5.5 %collective-permute-start.11 = (f32[40,256]{1,0:T(8,128)S(1)}, f32[40,256]{1,0:T(8,128)S(1)}, u32[]{:S(2)}, u32[]{:S(2)}) collective-permute-start(f32[40,256]{1,0:T(8,128)S(1)} %get-tuple-element.22.own.refs_9_), channel_id=1, source_target_pairs={{4,8},{8,4},{12,16},{16,12},{20,24},{24,20},{28,32},{32,28},{36,40... | collective-permute-start | bytes 122888 | tf_op jit(solution)/shard_map/ppermute | solution.py:62
  60.1 5.0 %collective-permute-start.15 = (f32[40,128]{1,0:T(8,128)S(1)}, f32[40,128]{1,0:T(8,128)S(1)}, u32[]{:S(2)}, u32[]{:S(2)}) collective-permute-start(f32[40,128]{1,0:T(8,128)S(1)} %broadcast_select_fusion.1), channel_id=1, source_target_pairs={{32,0},{36,4},{0,32},{4,36},{96,64},{100,68},{64,96},{68,100},{160... | collective-permute-start | bytes 61448 | tf_op jit(solution)/shard_map/ppermute | solution.py:35
  66.5 9.5 %collective-permute-start.19 = (f32[40,128]{1,0:T(8,128)S(1)}, f32[40,128]{1,0:T(8,128)S(1)}, u32[]{:S(2)}, u32[]{:S(2)}) collective-permute-start(f32[40,128]{1,0:T(8,128)S(1)} %add_select_fusion.3), channel_id=1, source_target_pairs={{160,0},{128,32},{224,64},{192,96},{32,128},{0,160},{96,192},{64,2... | collective-permute-start | bytes 61448 | tf_op jit(solution)/shard_map/ppermute | solution.py:35
  90.5 11.1 %collective-permute-start.23 = (f32[40,256]{1,0:T(8,128)S(1)}, f32[40,256]{1,0:T(8,128)S(1)}, u32[]{:S(2)}, u32[]{:S(2)}) collective-permute-start(f32[40,256]{1,0:T(8,128)S(1)} %get-tuple-element.27.own.refs_9_), channel_id=1, source_target_pairs={{8,0},{12,4},{16,8},{20,12},{24,16},{28,20},{32,24},{36,28},{40,32... | collective-permute-start | bytes 122888 | tf_op jit(solution)/shard_map/ppermute | solution.py:27
  91.8 9.9 %collective-permute-start.22 = (f32[40,256]{1,0:T(8,128)S(1)}, f32[40,256]{1,0:T(8,128)S(1)}, u32[]{:S(2)}, u32[]{:S(2)}) collective-permute-start(f32[40,256]{1,0:T(8,128)S(1)} %get-tuple-element.27.own.refs_9_), channel_id=1, source_target_pairs={{0,8},{4,12},{8,16},{12,20},{16,24},{20,28},{24,32},{28,36},{32,40... | collective-permute-start | bytes 122888 | tf_op jit(solution)/shard_map/ppermute | solution.py:27
  95.8 7.4 %collective-permute-start.21 = (f32[40,256]{1,0:T(8,128)S(1)}, f32[40,256]{1,0:T(8,128)S(1)}, u32[]{:S(2)}, u32[]{:S(2)}) collective-permute-start(f32[40,256]{1,0:T(8,128)S(1)} %get-tuple-element.27.own.refs_9_), channel_id=1, source_target_pairs={{4,8},{8,4},{12,16},{16,12},{20,24},{24,20},{28,32},{32,28},{36,40... | collective-permute-start | bytes 122888 | tf_op jit(solution)/shard_map/ppermute | solution.py:62
  104.3 4.8 %collective-permute-start.25 = (f32[40,128]{1,0:T(8,128)S(1)}, f32[40,128]{1,0:T(8,128)S(1)}, u32[]{:S(2)}, u32[]{:S(2)}) collective-permute-start(f32[40,128]{1,0:T(8,128)S(1)} %broadcast_select_fusion), channel_id=1, source_target_pairs={{32,0},{36,4},{0,32},{4,36},{96,64},{100,68},{64,96},{68,100},{160... | collective-permute-start | bytes 61448 | tf_op jit(solution)/shard_map/ppermute | solution.py:35
  104.4 6.0 %collective-permute-start.26 = (f32[40,128]{1,0:T(8,128)S(1)}, f32[40,128]{1,0:T(8,128)S(1)}, u32[]{:S(2)}, u32[]{:S(2)}) collective-permute-start(f32[40,128]{1,0:T(8,128)S(1)} %broadcast_select_fusion), channel_id=1, source_target_pairs={{36,0},{32,4},{4,32},{0,36},{100,64},{96,68},{68,96},{64,100},{164... | collective-permute-start | bytes 61448 | tf_op jit(solution)/shard_map/ppermute | solution.py:35
  110.5 6.0 %collective-permute-start.29 = (f32[40,128]{1,0:T(8,128)S(1)}, f32[40,128]{1,0:T(8,128)S(1)}, u32[]{:S(2)}, u32[]{:S(2)}) collective-permute-start(f32[40,128]{1,0:T(8,128)S(1)} %add_select_fusion.1), channel_id=1, source_target_pairs={{160,0},{128,32},{224,64},{192,96},{32,128},{0,160},{96,192},{64,2... | collective-permute-start | bytes 61448 | tf_op jit(solution)/shard_map/ppermute | solution.py:35
  131.3 10.8 %collective-permute-start.33 = (f32[40,256]{1,0:T(8,128)S(1)}, f32[40,256]{1,0:T(8,128)S(1)}, u32[]{:S(2)}, u32[]{:S(2)}) collective-permute-start(f32[40,256]{1,0:T(8,128)S(1)} %get-tuple-element.37.own), channel_id=1, source_target_pairs={{8,0},{12,4},{16,8},{20,12},{24,16},{28,20},{32,24},{36,28},{40,32... | collective-permute-start | bytes 122888 | tf_op jit(solution)/shard_map/ppermute | solution.py:27
  132.6 9.5 %collective-permute-start.32 = (f32[40,256]{1,0:T(8,128)S(1)}, f32[40,256]{1,0:T(8,128)S(1)}, u32[]{:S(2)}, u32[]{:S(2)}) collective-permute-start(f32[40,256]{1,0:T(8,128)S(1)} %get-tuple-element.37.own), channel_id=1, source_target_pairs={{0,8},{4,12},{8,16},{12,20},{16,24},{20,28},{24,32},{28,36},{32,40... | collective-permute-start | bytes 122888 | tf_op jit(solution)/shard_map/ppermute | solution.py:27
  136.6 7.1 %collective-permute-start.31 = (f32[40,256]{1,0:T(8,128)S(1)}, f32[40,256]{1,0:T(8,128)S(1)}, u32[]{:S(2)}, u32[]{:S(2)}) collective-permute-start(f32[40,256]{1,0:T(8,128)S(1)} %get-tuple-element.37.own), channel_id=1, source_target_pairs={{4,8},{8,4},{12,16},{16,12},{20,24},{24,20},{28,32},{32,28},{36,40... | collective-permute-start | bytes 122888 | tf_op jit(solution)/shard_map/ppermute | solution.py:62
  145.4 25.0 %all-to-all-start.3 = ((f32[256,1,128]{2,1,0:T(1,128)}), f32[256,1,128]{2,1,0:T(1,128)S(1)}, u32[]{:S(2)}, u32[]{:S(2)}) async-start(f32[256,1,128]{2,1,0:T(1,128)} %bitcast.19), calls=%async_computation.3 | async-start | bytes 262144 | tf_op jit(solution)/shard_map/all_to_all | solution.py:223
  (21 other events, 134.0 us)

commit v3 on v2

--- a/solution.py
+++ b/solution.py
@@ -23,8 +23,7 @@
 
 def shifted(value, axis, steps):
     count = lax.axis_size(axis)
-    first, last = (max(0, -steps), min(count, count - steps))
-    return lax.ppermute(value, axis, [(source, source + steps) for source in range(first, last)])
+    return lax.ppermute(value, axis, [(source, (source + steps) % count) for source in range(count)])
 
 
 def exchanged(value, axes, sources):
@@ -45,21 +44,23 @@
 ]
 
 
-def gathered(value, combine):
+def gathered(value, combine, later=None):
     value = combine(exchanged(value, ("agents_0", "agents_2"), PAIRS))
     value = combine(exchanged(value, ("agents_0",), OTHERS))
+    if later is not None:
+        value, later = lax.optimization_barrier((value, later))
     axes = ("agents_1", "group")
     every = jnp.broadcast_to(value[None], (lax.axis_size(axes), *value.shape))
-    return lax.all_to_all(every, axes, 0, 0, tiled=True)
+    return lax.all_to_all(every, axes, 0, 0, tiled=True), later
 
 
 def neighbours(field):
     count = lax.axis_size(AGENTS)
-    near = [(k, k + 1 if k % 2 else k - 1) for k in range(count)]
+    near = [(k, (k + 1 if k % 2 else k - 1) % count) for k in range(count)]
     return (
         field,
         lax.ppermute(field, "agents_2", [(0, 1), (1, 0)]),
-        lax.ppermute(field, AGENTS, [(a, b) for a, b in near if 0 <= b < count]),
+        lax.ppermute(field, AGENTS, near),
         shifted(field, AGENTS, 2),
         shifted(field, AGENTS, -2),
     )
@@ -196,7 +197,7 @@
     sums = jnp.einsum("ta,pa->tp", free_traj, onehot, precision=lax.Precision.HIGHEST)
     counts = jnp.sum(onehot, axis=1)[None]
     packed = jnp.concatenate([sums, counts, jnp.zeros((7, NPLAT), jnp.float32)])
-    parts = gathered(packed, added)
+    parts, traj = gathered(packed, added, free_traj)
     parts = parts.reshape(-1, *packed.shape)
     counts = jnp.sum(parts[:, traj_len], axis=0, keepdims=True)
     unused = counts < 0.5
@@ -204,7 +205,6 @@
     def joined(pieces):
         return jnp.where(unused, functools.reduce(jnp.maximum, pieces), added(pieces))
 
-    traj = free_traj
     _, total, _ = gaps(column, offsets, neighbours(traj), 8)
     new_multipliers = multipliers
     for step in range(ITERS):
@@ -218,7 +218,7 @@
         gap, total, peak = gaps(column, offsets, neighbours(traj), 8 if more else count)
         if more:
             packed = jnp.where(unused, peak[:1], sums)
-            parts = gathered(packed, joined).reshape(-1, *packed.shape)
+            parts = gathered(packed, joined)[0].reshape(-1, *packed.shape)
         else:
             peak = jnp.max(lax.all_to_all(peak, AGENTS_GROUP, 0, 0, tiled=True))
             new_multipliers = new_multipliers + gap / (1.0 + peak)

time: 175 us -> 156 us (0.89)
  starting transfers between devices: 101 us -> 86.1 us
  waiting for transfers between devices: 31 us -> 25.6 us
  blocking collectives: 22.9 us -> 25 us
    ppermute x12, starting transfers between devices: 41 us -> 22 us  [the longest x8 14.5 us: shifted(): lax.ppermute(value, axis, [(source, (source + steps) % count) for source...]
    ppermute x4, starting transfers between devices: 0.37 us -> 13 us  [neighbours(): lax.ppermute(field, 'agents_2', [(0, 1), (1, 0)])]
    all_to_all x1, waiting for transfers between devices: 7.19 us -> 0.01 us  [gathered(): return (lax.all_to_all(every, axes, 0, 0, tiled=True), later)]
    ppermute x18, starting transfers between devices: 38.4 us -> 34.4 us  [exchanged(): lax.ppermute(value, axes, [(at[source(*place)], at[place]) for place in p...]
    all_to_all x1, starting transfers between devices: 12.3 us -> 9.73 us  [local(): peak = jnp.max(lax.all_to_all(peak, AGENTS_GROUP, 0, 0, tiled=True))]
    ppermute x18, waiting for transfers between devices: 7.6 us -> 9.94 us  [exchanged(): lax.ppermute(value, axes, [(at[source(*place)], at[place]) for place in p...]
    all_to_all x2, blocking collectives: 22.9 us -> 25 us  [gathered(): return (lax.all_to_all(every, axes, 0, 0, tiled=True), later)]
    all_to_all x1, starting transfers between devices: 8.7 us -> 6.89 us  [gathered(): return (lax.all_to_all(every, axes, 0, 0, tiled=True), later)]
  transfers between devices with their start and end apart: 36 -> 36, of which waited for: 10 -> 12; matrix products, arithmetic and copies ran while one was open for 1% -> 1% of each run, Pallas kernels for 1% -> 1%
where the time goes in v3:
time: 156 us
  starting transfers between devices  86.1 us (55%)
  waiting for transfers between devices  25.6 us (16%)
  blocking collectives  25 us (16%)
  Pallas kernels  10.3 us (7%)
  other arithmetic  3.39 us (2%)
  local copies, waits for them, and re-layouts  2.73 us (2%)
  between operations  1.59 us (1%)
    ppermute x18, starting transfers between devices, exchanged(): lax.ppermute(value, axes, [(at[source(*place)], at[place]) for place in p...  34.4 us
    all_to_all x2, blocking collectives, gathered(): return (lax.all_to_all(every, axes, 0, 0, tiled=True), later)  25 us
    ppermute x8, starting transfers between devices, shifted(): lax.ppermute(value, axis, [(source, (source + steps) % count) for source...  14.5 us
    ppermute x4, starting transfers between devices, neighbours(): lax.ppermute(field, 'agents_2', [(0, 1), (1, 0)])  13 us
    all_to_all x1, waiting for transfers between devices, local(): peak = jnp.max(lax.all_to_all(peak, AGENTS_GROUP, 0, 0, tiled=True))  11.7 us
    ppermute x18, waiting for transfers between devices, exchanged(): lax.ppermute(value, axes, [(at[source(*place)], at[place]) for place in p...  9.94 us
    all_to_all x1, starting transfers between devices, local(): peak = jnp.max(lax.all_to_all(peak, AGENTS_GROUP, 0, 0, tiled=True))  9.73 us
    ppermute x4, starting transfers between devices, neighbours(): lax.ppermute(field, AGENTS, near)  7.54 us
  transfers between devices with their start and end apart: 36, of which 12 were waited for; matrix products, arithmetic and copies ran while one was open for 1% of the time, Pallas kernels for 1%

profile of v3, /device:TPU:1, one launch (start us, length us, event | category | flops | bytes accessed | tf_op | source)
XLA Modules:
  0.0 155.7 jit_solution(14362120896512593857)
XLA Ops:
  2.6 2.5 %collective-permute-start.1 = (f32[48,128]{1,0:T(8,128)S(1)}, f32[48,128]{1,0:T(8,128)S(1)}, u32[]{:S(2)}, u32[]{:S(2)}) collective-permute-start(f32[48,128]{1,0:T(8,128)S(1)} %maximum_maximum_fusion), channel_id=1, source_target_pairs={{32,0},{36,4},{0,32},{4,36},{96,64},{100,68},{64,96},{68,100},{160... | collective-permute-start | bytes 73736 | tf_op jit(solution)/shard_map/ppermute | solution.py:34
  5.1 2.4 %collective-permute-start.2 = (f32[48,128]{1,0:T(8,128)S(1)}, f32[48,128]{1,0:T(8,128)S(1)}, u32[]{:S(2)}, u32[]{:S(2)}) collective-permute-start(f32[48,128]{1,0:T(8,128)S(1)} %maximum_maximum_fusion), channel_id=1, source_target_pairs={{36,0},{32,4},{4,32},{0,36},{100,64},{96,68},{68,96},{64,100},{164... | collective-permute-start | bytes 73736 | tf_op jit(solution)/shard_map/ppermute | solution.py:34
  9.3 5.2 %collective-permute-start.5 = (f32[48,128]{1,0:T(8,128)S(1)}, f32[48,128]{1,0:T(8,128)S(1)}, u32[]{:S(2)}, u32[]{:S(2)}) collective-permute-start(f32[48,128]{1,0:T(8,128)S(1)} %add_add_fusion.1), channel_id=1, source_target_pairs={{160,0},{128,32},{224,64},{192,96},{32,128},{0,160},{96,192},{64,2... | collective-permute-start | bytes 73736 | tf_op jit(solution)/shard_map/ppermute | solution.py:34
  14.5 3.1 %collective-permute-start.3 = (f32[48,128]{1,0:T(8,128)S(1)}, f32[48,128]{1,0:T(8,128)S(1)}, u32[]{:S(2)}, u32[]{:S(2)}) collective-permute-start(f32[48,128]{1,0:T(8,128)S(1)} %add_add_fusion.1), channel_id=1, source_target_pairs={{224,0},{64,32},{32,64},{128,96},{96,128},{192,160},{160,192},{0,2... | collective-permute-start | bytes 73736 | tf_op jit(solution)/shard_map/ppermute | solution.py:34
  19.9 6.9 %all-to-all-start = ((f32[16,48,128]{2,1,0:T(8,128)}), f32[16,48,128]{2,1,0:T(8,128)S(1)}, u32[]{:S(2)}, u32[]{:S(2)}) async-start(f32[16,48,128]{2,1,0:T(8,128)} %broadcast_in_dim.111), calls=%async_computation | async-start | bytes 786432 | tf_op jit(solution)/shard_map/all_to_all | solution.py:54
  26.9 4.8 %collective-permute-start.9 = (f32[40,256]{1,0:T(8,128)S(1)}, f32[40,256]{1,0:T(8,128)S(1)}, u32[]{:S(2)}, u32[]{:S(2)}) collective-permute-start(f32[40,256]{1,0:T(8,128)S(1)} %bitcast.51), channel_id=1, source_target_pairs={{0,248},{4,252},{8,0},{12,4},{16,8},{20,12},{24,16},{28,20},{32,24... | collective-permute-start | bytes 122888 | tf_op jit(solution)/shard_map/ppermute | solution.py:26
  32.8 4.0 %collective-permute-start.6 = (f32[40,256]{1,0:T(8,128)S(1)}, f32[40,256]{1,0:T(8,128)S(1)}, u32[]{:S(2)}, u32[]{:S(2)}) collective-permute-start(f32[40,256]{1,0:T(8,128)S(1)} %bitcast.54), channel_id=1, source_target_pairs={{0,4},{4,0},{1,5},{5,1},{2,6},{6,2},{3,7},{7,3},{8,12},{12,8},{9,1... | collective-permute-start | bytes 122888 | tf_op jit(solution)/shard_map/ppermute | solution.py:62
  41.1 5.3 %collective-permute-start.13 = (f32[40,256]{1,0:T(8,128)S(1)}, f32[40,256]{1,0:T(8,128)S(1)}, u32[]{:S(2)}, u32[]{:S(2)}) collective-permute-start(f32[40,256]{1,0:T(8,128)S(1)} %get-tuple-element.26.own.refs_9_), channel_id=1, source_target_pairs={{0,248},{4,252},{8,0},{12,4},{16,8},{20,12},{24,16},{28,20},{32,24... | collective-permute-start | bytes 122888 | tf_op jit(solution)/shard_map/ppermute | solution.py:26
  47.0 4.6 %collective-permute-start.10 = (f32[40,256]{1,0:T(8,128)S(1)}, f32[40,256]{1,0:T(8,128)S(1)}, u32[]{:S(2)}, u32[]{:S(2)}) collective-permute-start(f32[40,256]{1,0:T(8,128)S(1)} %get-tuple-element.26.own.refs_9_), channel_id=1, source_target_pairs={{0,4},{4,0},{1,5},{5,1},{2,6},{6,2},{3,7},{7,3},{8,12},{12,8},{9,1... | collective-permute-start | bytes 122888 | tf_op jit(solution)/shard_map/ppermute | solution.py:62
  54.1 3.6 %collective-permute-start.16 = (f32[40,128]{1,0:T(8,128)S(1)}, f32[40,128]{1,0:T(8,128)S(1)}, u32[]{:S(2)}, u32[]{:S(2)}) collective-permute-start(f32[40,128]{1,0:T(8,128)S(1)} %broadcast_select_fusion.1), channel_id=1, source_target_pairs={{36,0},{32,4},{4,32},{0,36},{100,64},{96,68},{68,96},{64,100},{164... | collective-permute-start | bytes 61448 | tf_op jit(solution)/shard_map/ppermute | solution.py:34
  57.6 1.8 %collective-permute-done.16 = f32[40,128]{1,0:T(8,128)S(1)} collective-permute-done((f32[40,128]{1,0:T(8,128)S(1)}, f32[40,128]{1,0:T(8,128)S(1)}, u32[]{:S(2)}, u32[]{:S(2)}) %collective-permute-start.16) | collective-permute-done | bytes 20512 | tf_op jit(solution)/shard_map/ppermute | solution.py:34
  59.7 3.8 %collective-permute-start.17 = (f32[40,128]{1,0:T(8,128)S(1)}, f32[40,128]{1,0:T(8,128)S(1)}, u32[]{:S(2)}, u32[]{:S(2)}) collective-permute-start(f32[40,128]{1,0:T(8,128)S(1)} %add_select_fusion.3), channel_id=1, source_target_pairs={{224,0},{64,32},{32,64},{128,96},{96,128},{192,160},{160,192},{0,2... | collective-permute-start | bytes 61448 | tf_op jit(solution)/shard_map/ppermute | solution.py:34
  65.3 14.6 %all_to_all.24.refs_0_ = f32[16,40,128]{2,1,0:T(8,128)S(1)} all-to-all(f32[16,40,128]{2,1,0:T(8,128)S(1)} %broadcast_in_dim.122), channel_id=1, replica_groups=mesh['agents_0'=8,'agents_1'=4,'agents_2'=2,'group'=4] {'agents_1','group'}, dimensions={0} | all-to-all | bytes 655360 | tf_op jit(solution)/shard_map/all_to_all | solution.py:54
  82.8 3.7 %collective-permute-start.21 = (f32[40,256]{1,0:T(8,128)S(1)}, f32[40,256]{1,0:T(8,128)S(1)}, u32[]{:S(2)}, u32[]{:S(2)}) collective-permute-start(f32[40,256]{1,0:T(8,128)S(1)} %get-tuple-element.31.own.refs_9_), channel_id=1, source_target_pairs={{0,252},{4,8},{8,4},{12,16},{16,12},{20,24},{24,20},{28,32},{32,28... | collective-permute-start | bytes 122888 | tf_op jit(solution)/shard_map/ppermute | solution.py:63
  90.1 6.3 %collective-permute-start.26 = (f32[40,128]{1,0:T(8,128)S(1)}, f32[40,128]{1,0:T(8,128)S(1)}, u32[]{:S(2)}, u32[]{:S(2)}) collective-permute-start(f32[40,128]{1,0:T(8,128)S(1)} %broadcast_select_fusion), channel_id=1, source_target_pairs={{36,0},{32,4},{4,32},{0,36},{100,64},{96,68},{68,96},{64,100},{164... | collective-permute-start | bytes 61448 | tf_op jit(solution)/shard_map/ppermute | solution.py:34
  98.1 2.9 %collective-permute-start.29 = (f32[40,128]{1,0:T(8,128)S(1)}, f32[40,128]{1,0:T(8,128)S(1)}, u32[]{:S(2)}, u32[]{:S(2)}) collective-permute-start(f32[40,128]{1,0:T(8,128)S(1)} %add_select_fusion.1), channel_id=1, source_target_pairs={{160,0},{128,32},{224,64},{192,96},{32,128},{0,160},{96,192},{64,2... | collective-permute-start | bytes 61448 | tf_op jit(solution)/shard_map/ppermute | solution.py:34
  102.1 3.1 %collective-permute-start.27 = (f32[40,128]{1,0:T(8,128)S(1)}, f32[40,128]{1,0:T(8,128)S(1)}, u32[]{:S(2)}, u32[]{:S(2)}) collective-permute-start(f32[40,128]{1,0:T(8,128)S(1)} %add_select_fusion.1), channel_id=1, source_target_pairs={{224,0},{64,32},{32,64},{128,96},{96,128},{192,160},{160,192},{0,2... | collective-permute-start | bytes 61448 | tf_op jit(solution)/shard_map/ppermute | solution.py:34
  106.6 10.4 %all_to_all.25.refs_0_ = f32[16,40,128]{2,1,0:T(8,128)S(1)} all-to-all(f32[16,40,128]{2,1,0:T(8,128)S(1)} %broadcast_in_dim.125), channel_id=1, replica_groups=mesh['agents_0'=8,'agents_1'=4,'agents_2'=2,'group'=4] {'agents_1','group'}, dimensions={0} | all-to-all | bytes 655360 | tf_op jit(solution)/shard_map/all_to_all | solution.py:54
  118.7 2.9 %collective-permute-start.33 = (f32[40,256]{1,0:T(8,128)S(1)}, f32[40,256]{1,0:T(8,128)S(1)}, u32[]{:S(2)}, u32[]{:S(2)}) collective-permute-start(f32[40,256]{1,0:T(8,128)S(1)} %get-tuple-element.41.own), channel_id=1, source_target_pairs={{0,248},{4,252},{8,0},{12,4},{16,8},{20,12},{24,16},{28,20},{32,24... | collective-permute-start | bytes 122888 | tf_op jit(solution)/shard_map/ppermute | solution.py:26
  121.6 2.2 %collective-permute-start.31 = (f32[40,256]{1,0:T(8,128)S(1)}, f32[40,256]{1,0:T(8,128)S(1)}, u32[]{:S(2)}, u32[]{:S(2)}) collective-permute-start(f32[40,256]{1,0:T(8,128)S(1)} %get-tuple-element.41.own), channel_id=1, source_target_pairs={{0,252},{4,8},{8,4},{12,16},{16,12},{20,24},{24,20},{28,32},{32,28... | collective-permute-start | bytes 122888 | tf_op jit(solution)/shard_map/ppermute | solution.py:63
  123.8 3.0 %collective-permute-start.30 = (f32[40,256]{1,0:T(8,128)S(1)}, f32[40,256]{1,0:T(8,128)S(1)}, u32[]{:S(2)}, u32[]{:S(2)}) collective-permute-start(f32[40,256]{1,0:T(8,128)S(1)} %get-tuple-element.41.own), channel_id=1, source_target_pairs={{0,4},{4,0},{1,5},{5,1},{2,6},{6,2},{3,7},{7,3},{8,12},{12,8},{9,1... | collective-permute-start | bytes 122888 | tf_op jit(solution)/shard_map/ppermute | solution.py:62
  129.5 9.7 %all-to-all-start.3 = ((f32[256,1,128]{2,1,0:T(1,128)}), f32[256,1,128]{2,1,0:T(1,128)S(1)}, u32[]{:S(2)}, u32[]{:S(2)}) async-start(f32[256,1,128]{2,1,0:T(1,128)} %bitcast.19), calls=%async_computation.3 | async-start | bytes 262144 | tf_op jit(solution)/shard_map/all_to_all | solution.py:223
  140.4 11.7 %all-to-all-done.3 = f32[256,1,128]{2,1,0:T(1,128)S(1)} async-done(((f32[256,1,128]{2,1,0:T(1,128)}), f32[256,1,128]{2,1,0:T(1,128)S(1)}, u32[]{:S(2)}, u32[]{:S(2)}) %all-to-all-start.3) | async-done | bytes 131104 | tf_op jit(solution)/shard_map/all_to_all | solution.py:223
  153.6 2.1 %fusion.3 = f32[1,8,40,256]{3,2,1,0:T(8,128)} fusion(f32[1,8,40,256]{3,2,1,0:T(8,128)S(1)} %copy-done.6, f32[8,40,256]{2,1,0:T(8,128)S(1)} %get-tuple-element.42, f32[8,40,256]{2,1,0:T(8,128)S(1)} %get-tuple-element.40, f32[8,40,256]{2,1,0:T(8,128)S(1)} %get-tuple-element.38, f32[]{:T(128)S(6)} %add_shard_map.3, f32[]{:T(128)} %bitcast.17, f32[]{:T(128)} %bitcast.16), kind=kLoop, calls=%fused_computation.6 | loop fusion | flops 491520 | bytes 1638412 | tf_op jit(solution)/shard_map/broadcast_in_dim | solution.py:225
  (102 shorter events, 33.5 us)
Async XLA Ops:
  9.3 8.3 %collective-permute-start.5 = (f32[48,128]{1,0:T(8,128)S(1)}, f32[48,128]{1,0:T(8,128)S(1)}, u32[]{:S(2)}, u32[]{:S(2)}) collective-permute-start(f32[48,128]{1,0:T(8,128)S(1)} %add_add_fusion.1), channel_id=1, source_target_pairs={{160,0},{128,32},{224,64},{192,96},{32,128},{0,160},{96,192},{64,2... | collective-permute-start | bytes 73736 | tf_op jit(solution)/shard_map/ppermute | solution.py:34
  19.9 19.7 %all-to-all-start = ((f32[16,48,128]{2,1,0:T(8,128)}), f32[16,48,128]{2,1,0:T(8,128)S(1)}, u32[]{:S(2)}, u32[]{:S(2)}) async-start(f32[16,48,128]{2,1,0:T(8,128)} %broadcast_in_dim.111), calls=%async_computation | async-start | bytes 786432 | tf_op jit(solution)/shard_map/all_to_all | solution.py:54
  26.9 10.0 %collective-permute-start.9 = (f32[40,256]{1,0:T(8,128)S(1)}, f32[40,256]{1,0:T(8,128)S(1)}, u32[]{:S(2)}, u32[]{:S(2)}) collective-permute-start(f32[40,256]{1,0:T(8,128)S(1)} %bitcast.51), channel_id=1, source_target_pairs={{0,248},{4,252},{8,0},{12,4},{16,8},{20,12},{24,16},{28,20},{32,24... | collective-permute-start | bytes 122888 | tf_op jit(solution)/shard_map/ppermute | solution.py:26
  31.7 6.2 %collective-permute-start.8 = (f32[40,256]{1,0:T(8,128)S(1)}, f32[40,256]{1,0:T(8,128)S(1)}, u32[]{:S(2)}, u32[]{:S(2)}) collective-permute-start(f32[40,256]{1,0:T(8,128)S(1)} %bitcast.52), channel_id=1, source_target_pairs={{0,8},{4,12},{8,16},{12,20},{16,24},{20,28},{24,32},{28,36},{32,40... | collective-permute-start | bytes 122888 | tf_op jit(solution)/shard_map/ppermute | solution.py:26
  31.7 6.2 %collective-permute-start.7 = (f32[40,256]{1,0:T(8,128)S(1)}, f32[40,256]{1,0:T(8,128)S(1)}, u32[]{:S(2)}, u32[]{:S(2)}) collective-permute-start(f32[40,256]{1,0:T(8,128)S(1)} %bitcast.53), channel_id=1, source_target_pairs={{0,252},{4,8},{8,4},{12,16},{16,12},{20,24},{24,20},{28,32},{32,28... | collective-permute-start | bytes 122888 | tf_op jit(solution)/shard_map/ppermute | solution.py:63
  32.8 5.0 %collective-permute-start.6 = (f32[40,256]{1,0:T(8,128)S(1)}, f32[40,256]{1,0:T(8,128)S(1)}, u32[]{:S(2)}, u32[]{:S(2)}) collective-permute-start(f32[40,256]{1,0:T(8,128)S(1)} %bitcast.54), channel_id=1, source_target_pairs={{0,4},{4,0},{1,5},{5,1},{2,6},{6,2},{3,7},{7,3},{8,12},{12,8},{9,1... | collective-permute-start | bytes 122888 | tf_op jit(solution)/shard_map/ppermute | solution.py:62
  41.1 10.5 %collective-permute-start.13 = (f32[40,256]{1,0:T(8,128)S(1)}, f32[40,256]{1,0:T(8,128)S(1)}, u32[]{:S(2)}, u32[]{:S(2)}) collective-permute-start(f32[40,256]{1,0:T(8,128)S(1)} %get-tuple-element.26.own.refs_9_), channel_id=1, source_target_pairs={{0,248},{4,252},{8,0},{12,4},{16,8},{20,12},{24,16},{28,20},{32,24... | collective-permute-start | bytes 122888 | tf_op jit(solution)/shard_map/ppermute | solution.py:26
  46.5 6.2 %collective-permute-start.12 = (f32[40,256]{1,0:T(8,128)S(1)}, f32[40,256]{1,0:T(8,128)S(1)}, u32[]{:S(2)}, u32[]{:S(2)}) collective-permute-start(f32[40,256]{1,0:T(8,128)S(1)} %get-tuple-element.26.own.refs_9_), channel_id=1, source_target_pairs={{0,8},{4,12},{8,16},{12,20},{16,24},{20,28},{24,32},{28,36},{32,40... | collective-permute-start | bytes 122888 | tf_op jit(solution)/shard_map/ppermute | solution.py:26
  46.5 6.2 %collective-permute-start.11 = (f32[40,256]{1,0:T(8,128)S(1)}, f32[40,256]{1,0:T(8,128)S(1)}, u32[]{:S(2)}, u32[]{:S(2)}) collective-permute-start(f32[40,256]{1,0:T(8,128)S(1)} %get-tuple-element.26.own.refs_9_), channel_id=1, source_target_pairs={{0,252},{4,8},{8,4},{12,16},{16,12},{20,24},{24,20},{28,32},{32,28... | collective-permute-start | bytes 122888 | tf_op jit(solution)/shard_map/ppermute | solution.py:63
  47.0 5.6 %collective-permute-start.10 = (f32[40,256]{1,0:T(8,128)S(1)}, f32[40,256]{1,0:T(8,128)S(1)}, u32[]{:S(2)}, u32[]{:S(2)}) collective-permute-start(f32[40,256]{1,0:T(8,128)S(1)} %get-tuple-element.26.own.refs_9_), channel_id=1, source_target_pairs={{0,4},{4,0},{1,5},{5,1},{2,6},{6,2},{3,7},{7,3},{8,12},{12,8},{9,1... | collective-permute-start | bytes 122888 | tf_op jit(solution)/shard_map/ppermute | solution.py:62
  54.1 5.4 %collective-permute-start.16 = (f32[40,128]{1,0:T(8,128)S(1)}, f32[40,128]{1,0:T(8,128)S(1)}, u32[]{:S(2)}, u32[]{:S(2)}) collective-permute-start(f32[40,128]{1,0:T(8,128)S(1)} %broadcast_select_fusion.1), channel_id=1, source_target_pairs={{36,0},{32,4},{4,32},{0,36},{100,64},{96,68},{68,96},{64,100},{164... | collective-permute-start | bytes 61448 | tf_op jit(solution)/shard_map/ppermute | solution.py:34
  59.5 5.7 %collective-permute-start.19 = (f32[40,128]{1,0:T(8,128)S(1)}, f32[40,128]{1,0:T(8,128)S(1)}, u32[]{:S(2)}, u32[]{:S(2)}) collective-permute-start(f32[40,128]{1,0:T(8,128)S(1)} %add_select_fusion.3), channel_id=1, source_target_pairs={{160,0},{128,32},{224,64},{192,96},{32,128},{0,160},{96,192},{64,2... | collective-permute-start | bytes 61448 | tf_op jit(solution)/shard_map/ppermute | solution.py:34
  59.6 5.6 %collective-permute-start.18 = (f32[40,128]{1,0:T(8,128)S(1)}, f32[40,128]{1,0:T(8,128)S(1)}, u32[]{:S(2)}, u32[]{:S(2)}) collective-permute-start(f32[40,128]{1,0:T(8,128)S(1)} %add_select_fusion.3), channel_id=1, source_target_pairs={{64,0},{224,32},{128,64},{32,96},{192,128},{96,160},{0,192},{160,2... | collective-permute-start | bytes 61448 | tf_op jit(solution)/shard_map/ppermute | solution.py:34
  59.7 5.5 %collective-permute-start.17 = (f32[40,128]{1,0:T(8,128)S(1)}, f32[40,128]{1,0:T(8,128)S(1)}, u32[]{:S(2)}, u32[]{:S(2)}) collective-permute-start(f32[40,128]{1,0:T(8,128)S(1)} %add_select_fusion.3), channel_id=1, source_target_pairs={{224,0},{64,32},{32,64},{128,96},{96,128},{192,160},{160,192},{0,2... | collective-permute-start | bytes 61448 | tf_op jit(solution)/shard_map/ppermute | solution.py:34
  81.4 6.5 %collective-permute-start.23 = (f32[40,256]{1,0:T(8,128)S(1)}, f32[40,256]{1,0:T(8,128)S(1)}, u32[]{:S(2)}, u32[]{:S(2)}) collective-permute-start(f32[40,256]{1,0:T(8,128)S(1)} %get-tuple-element.31.own.refs_9_), channel_id=1, source_target_pairs={{0,248},{4,252},{8,0},{12,4},{16,8},{20,12},{24,16},{28,20},{32,24... | collective-permute-start | bytes 122888 | tf_op jit(solution)/shard_map/ppermute | solution.py:26
  82.7 6.2 %collective-permute-start.22 = (f32[40,256]{1,0:T(8,128)S(1)}, f32[40,256]{1,0:T(8,128)S(1)}, u32[]{:S(2)}, u32[]{:S(2)}) collective-permute-start(f32[40,256]{1,0:T(8,128)S(1)} %get-tuple-element.31.own.refs_9_), channel_id=1, source_target_pairs={{0,8},{4,12},{8,16},{12,20},{16,24},{20,28},{24,32},{28,36},{32,40... | collective-permute-start | bytes 122888 | tf_op jit(solution)/shard_map/ppermute | solution.py:26
  82.8 6.0 %collective-permute-start.21 = (f32[40,256]{1,0:T(8,128)S(1)}, f32[40,256]{1,0:T(8,128)S(1)}, u32[]{:S(2)}, u32[]{:S(2)}) collective-permute-start(f32[40,256]{1,0:T(8,128)S(1)} %get-tuple-element.31.own.refs_9_), channel_id=1, source_target_pairs={{0,252},{4,8},{8,4},{12,16},{16,12},{20,24},{24,20},{28,32},{32,28... | collective-permute-start | bytes 122888 | tf_op jit(solution)/shard_map/ppermute | solution.py:63
  90.0 6.4 %collective-permute-start.25 = (f32[40,128]{1,0:T(8,128)S(1)}, f32[40,128]{1,0:T(8,128)S(1)}, u32[]{:S(2)}, u32[]{:S(2)}) collective-permute-start(f32[40,128]{1,0:T(8,128)S(1)} %broadcast_select_fusion), channel_id=1, source_target_pairs={{32,0},{36,4},{0,32},{4,36},{96,64},{100,68},{64,96},{68,100},{160... | collective-permute-start | bytes 61448 | tf_op jit(solution)/shard_map/ppermute | solution.py:34
  90.1 8.0 %collective-permute-start.26 = (f32[40,128]{1,0:T(8,128)S(1)}, f32[40,128]{1,0:T(8,128)S(1)}, u32[]{:S(2)}, u32[]{:S(2)}) collective-permute-start(f32[40,128]{1,0:T(8,128)S(1)} %broadcast_select_fusion), channel_id=1, source_target_pairs={{36,0},{32,4},{4,32},{0,36},{100,64},{96,68},{68,96},{64,100},{164... | collective-permute-start | bytes 61448 | tf_op jit(solution)/shard_map/ppermute | solution.py:34
  98.1 7.0 %collective-permute-start.29 = (f32[40,128]{1,0:T(8,128)S(1)}, f32[40,128]{1,0:T(8,128)S(1)}, u32[]{:S(2)}, u32[]{:S(2)}) collective-permute-start(f32[40,128]{1,0:T(8,128)S(1)} %add_select_fusion.1), channel_id=1, source_target_pairs={{160,0},{128,32},{224,64},{192,96},{32,128},{0,160},{96,192},{64,2... | collective-permute-start | bytes 61448 | tf_op jit(solution)/shard_map/ppermute | solution.py:34
  118.7 8.1 %collective-permute-start.33 = (f32[40,256]{1,0:T(8,128)S(1)}, f32[40,256]{1,0:T(8,128)S(1)}, u32[]{:S(2)}, u32[]{:S(2)}) collective-permute-start(f32[40,256]{1,0:T(8,128)S(1)} %get-tuple-element.41.own), channel_id=1, source_target_pairs={{0,248},{4,252},{8,0},{12,4},{16,8},{20,12},{24,16},{28,20},{32,24... | collective-permute-start | bytes 122888 | tf_op jit(solution)/shard_map/ppermute | solution.py:26
  121.6 6.2 %collective-permute-start.32 = (f32[40,256]{1,0:T(8,128)S(1)}, f32[40,256]{1,0:T(8,128)S(1)}, u32[]{:S(2)}, u32[]{:S(2)}) collective-permute-start(f32[40,256]{1,0:T(8,128)S(1)} %get-tuple-element.41.own), channel_id=1, source_target_pairs={{0,8},{4,12},{8,16},{12,20},{16,24},{20,28},{24,32},{28,36},{32,40... | collective-permute-start | bytes 122888 | tf_op jit(solution)/shard_map/ppermute | solution.py:26
  121.6 6.2 %collective-permute-start.31 = (f32[40,256]{1,0:T(8,128)S(1)}, f32[40,256]{1,0:T(8,128)S(1)}, u32[]{:S(2)}, u32[]{:S(2)}) collective-permute-start(f32[40,256]{1,0:T(8,128)S(1)} %get-tuple-element.41.own), channel_id=1, source_target_pairs={{0,252},{4,8},{8,4},{12,16},{16,12},{20,24},{24,20},{28,32},{32,28... | collective-permute-start | bytes 122888 | tf_op jit(solution)/shard_map/ppermute | solution.py:63
  129.5 22.5 %all-to-all-start.3 = ((f32[256,1,128]{2,1,0:T(1,128)}), f32[256,1,128]{2,1,0:T(1,128)S(1)}, u32[]{:S(2)}, u32[]{:S(2)}) async-start(f32[256,1,128]{2,1,0:T(1,128)} %bitcast.19), calls=%async_computation.3 | async-start | bytes 262144 | tf_op jit(solution)/shard_map/all_to_all | solution.py:223
  (21 other events, 153.0 us)

commit v4 on v3

--- a/solution.py
+++ b/solution.py
@@ -9,7 +9,6 @@
 from jax.sharding import Mesh
 from jax.sharding import PartitionSpec as P
 
-SPAN = 2
 NPLAT = 128
 ITERS = 3
 LANES = 128
@@ -44,14 +43,14 @@
 ]
 
 
-def gathered(value, combine, later=None):
+def gathered(value, combine, ready=None):
     value = combine(exchanged(value, ("agents_0", "agents_2"), PAIRS))
     value = combine(exchanged(value, ("agents_0",), OTHERS))
-    if later is not None:
-        value, later = lax.optimization_barrier((value, later))
+    if ready is not None:
+        value, ready = lax.optimization_barrier((value, ready))
     axes = ("agents_1", "group")
     every = jnp.broadcast_to(value[None], (lax.axis_size(axes), *value.shape))
-    return lax.all_to_all(every, axes, 0, 0, tiled=True), later
+    return lax.all_to_all(every, axes, 0, 0, tiled=True), ready
 
 
 def neighbours(field):
@@ -67,7 +66,7 @@
 
 
 def gap_kernel(column, offsets, own, *rest):
-    fields, (gap, total, peak) = ((own, *rest[:4]), rest[4:])
+    fields, (total, *kept) = ((own, *rest[:4]), rest[4:])
     degree, length, block = offsets.shape
     wide = (length, LANES)
     largest = jnp.zeros(wide, jnp.float32)
@@ -88,22 +87,23 @@
             value = jnp.where(
                 index >= 0, here - near - offsets[k, :, first : first + LANES], 0.0
             )
-            gap[k, :, first : first + LANES] = value
             added += value
-            largest = jnp.maximum(largest, jnp.abs(value))
+            if kept:
+                kept[0][k, :, first : first + LANES] = value
+                largest = jnp.maximum(largest, jnp.abs(value))
         total[:, first : first + LANES] = added
-    peak[...] = jnp.broadcast_to(jnp.max(largest), peak.shape)
+    if kept:
+        kept[1][...] = jnp.broadcast_to(jnp.max(largest), kept[1].shape)
 
 
 def gaps(column, offsets, fields, rows):
     degree, length, block = offsets.shape
+    shapes = [(length, block), (degree, length, block), (rows, LANES)]
     return pl.pallas_call(
         gap_kernel,
-        out_shape=(
-            jax.ShapeDtypeStruct((degree, length, block), jnp.float32),
-            jax.ShapeDtypeStruct((length, block), jnp.float32),
-            jax.ShapeDtypeStruct((rows, LANES), jnp.float32),
-        ),
+        out_shape=[
+            jax.ShapeDtypeStruct(shape, jnp.float32) for shape in shapes[: 3 if rows else 1]
+        ],
         compiler_params=pltpu.CompilerParams(vmem_limit_bytes=16 * 1024 * 1024),
         name="gaps",
     )(column, offsets, *fields)
@@ -167,12 +167,25 @@
             jax.ShapeDtypeStruct((qp, block), jnp.float32),
             jax.ShapeDtypeStruct((length, block), jnp.float32),
             jax.ShapeDtypeStruct((length, NPLAT), jnp.float32),
-            jax.ShapeDtypeStruct((8, LANES), jnp.float32),
+            jax.ShapeDtypeStruct((length, block), jnp.float32),
             jax.ShapeDtypeStruct((length, block), jnp.float32),
         ),
         compiler_params=pltpu.CompilerParams(vmem_limit_bytes=16 * 1024 * 1024),
         name="solve",
     )(*args)
+
+
+def finish_kernel(peaks, before, gap, out):
+    out[...] = before[...] + gap[...] * (1.0 / (1.0 + jnp.max(peaks[...])))
+
+
+def finished(peaks, before, gap):
+    return pl.pallas_call(
+        finish_kernel,
+        out_shape=jax.ShapeDtypeStruct(gap.shape, jnp.float32),
+        compiler_params=pltpu.CompilerParams(vmem_limit_bytes=16 * 1024 * 1024),
+        name="finish",
+    )(peaks, before, gap)
 
 
 def added(pieces):
@@ -197,7 +210,10 @@
     sums = jnp.einsum("ta,pa->tp", free_traj, onehot, precision=lax.Precision.HIGHEST)
     counts = jnp.sum(onehot, axis=1)[None]
     packed = jnp.concatenate([sums, counts, jnp.zeros((7, NPLAT), jnp.float32)])
-    parts, traj = gathered(packed, added, free_traj)
+    fields = neighbours(free_traj)
+    (total,) = gaps(column, offsets, fields, 0)
+    parts, (total, lam, column, alive) = gathered(packed, added, (total, lam, column, alive))
+    traj = free_traj
     parts = parts.reshape(-1, *packed.shape)
     counts = jnp.sum(parts[:, traj_len], axis=0, keepdims=True)
     unused = counts < 0.5
@@ -205,23 +221,23 @@
     def joined(pieces):
         return jnp.where(unused, functools.reduce(jnp.maximum, pieces), added(pieces))
 
-    _, total, _ = gaps(column, offsets, neighbours(traj), 8)
     new_multipliers = multipliers
     for step in range(ITERS):
         plan, traj, sums, scale, lam = solved(
             step == 0, parts, counts, platoon, q_lin, inverse, predict, free_traj, lam, total, traj, alive
         )
         if step > 0:
-            new_multipliers = new_multipliers + scale[0, 0] * gap
+            new_multipliers = new_multipliers + scale[None] * gap
         more = step + 1 < ITERS
         count = lax.axis_size(AGENTS_GROUP)
-        gap, total, peak = gaps(column, offsets, neighbours(traj), 8 if more else count)
+        total, gap, peak = gaps(column, offsets, neighbours(traj), 8 if more else count)
         if more:
             packed = jnp.where(unused, peak[:1], sums)
             parts = gathered(packed, joined)[0].reshape(-1, *packed.shape)
         else:
-            peak = jnp.max(lax.all_to_all(peak, AGENTS_GROUP, 0, 0, tiled=True))
-            new_multipliers = new_multipliers + gap / (1.0 + peak)
+            peak, new_multipliers = lax.optimization_barrier((peak, new_multipliers))
+            peaks = lax.all_to_all(peak, AGENTS_GROUP, 0, 0, tiled=True)
+            new_multipliers = finished(peaks, new_multipliers, gap)
     return (plan[None], new_multipliers[None])
 
 

time: 156 us -> 150 us (0.962)
  blocking collectives: 25 us -> 57.1 us
  starting transfers between devices: 86.1 us -> 67.3 us
  waiting for transfers between devices: 25.6 us -> 10.2 us
  other arithmetic: 3.39 us -> 1.51 us
  local copies, waits for them, and re-layouts: 2.73 us -> 0.88 us
    all_to_all x2 -> x4, blocking collectives: 25 us -> 57.1 us  [the longest x3 33.5 us: gathered(): return (lax.all_to_all(every, axes, 0, 0, tiled=True), ready)]
    all_to_all x2 -> x0, starting transfers between devices: 16.6 us -> none  [the longest x1 9.73 us: local(): peak = jnp.max(lax.all_to_all(peak, AGENTS_GROUP, 0, 0, tiled=True))]
    all_to_all x2 -> x0, waiting for transfers between devices: 11.7 us -> none  [the longest x1 11.7 us: local(): peak = jnp.max(lax.all_to_all(peak, AGENTS_GROUP, 0, 0, tiled=True))]
    ppermute x18, waiting for transfers between devices: 9.94 us -> 7.03 us  [exchanged(): lax.ppermute(value, axes, [(at[source(*place)], at[place]) for place in p...]
    broadcast_in_dim x1 -> x0, other arithmetic: 2.09 us -> none  [local(): return (plan[None], new_multipliers[None])]
    ppermute x18, starting transfers between devices: 34.4 us -> 32.4 us  [exchanged(): lax.ppermute(value, axes, [(at[source(*place)], at[place]) for place in p...]
    pallas_call x4 -> x5, Pallas kernels: 5.66 us -> 5.72 us  [the longest x4 4.79 us: gaps(): pl.pallas_call(gap_kernel, out_shape=[jax.ShapeDtypeStruct(shape, jnp.flo...]
  transfers between devices with their start and end apart: 36 -> 34, of which waited for: 12 -> 10; matrix products, arithmetic and copies ran while one was open for 1% -> 1% of each run, Pallas kernels for 1% -> 1%
where the time goes in v4:
time: 150 us; the launch traced here: 149 us
  starting transfers between devices  67.3 us (45%)
  blocking collectives  57.1 us (38%)
  Pallas kernels  10.4 us (7%)
  waiting for transfers between devices  10.2 us (7%)
  other arithmetic  1.51 us (1%)
    all_to_all x3, blocking collectives, gathered(): return (lax.all_to_all(every, axes, 0, 0, tiled=True), ready)  33.5 us
    ppermute x18, starting transfers between devices, exchanged(): lax.ppermute(value, axes, [(at[source(*place)], at[place]) for place in p...  32.4 us
    all_to_all x1, blocking collectives, local(): peaks = lax.all_to_all(peak, AGENTS_GROUP, 0, 0, tiled=True)  23.6 us
    ppermute x8, starting transfers between devices, shifted(): lax.ppermute(value, axis, [(source, (source + steps) % count) for source...  14.1 us
    ppermute x4, starting transfers between devices, neighbours(): lax.ppermute(field, 'agents_2', [(0, 1), (1, 0)])  13 us
    ppermute x4, starting transfers between devices, neighbours(): lax.ppermute(field, AGENTS, near)  7.82 us
    ppermute x18, waiting for transfers between devices, exchanged(): lax.ppermute(value, axes, [(at[source(*place)], at[place]) for place in p...  7.03 us
    pallas_call x4, Pallas kernels, gaps(): pl.pallas_call(gap_kernel, out_shape=[jax.ShapeDtypeStruct(shape, jnp.flo...  4.79 us
  transfers between devices with their start and end apart: 34, of which 10 were waited for; matrix products, arithmetic and copies ran while one was open for 1% of the time, Pallas kernels for 1%

profile of v4, /device:TPU:1, one launch (start us, length us, event | category | flops | bytes accessed | tf_op | source)
XLA Modules:
  0.0 149.3 jit_solution(327703124431314336)
XLA Ops:
  2.7 2.5 %collective-permute-start.1 = (f32[48,128]{1,0:T(8,128)S(1)}, f32[48,128]{1,0:T(8,128)S(1)}, u32[]{:S(2)}, u32[]{:S(2)}) collective-permute-start(f32[48,128]{1,0:T(8,128)S(1)} %maximum_maximum_fusion), channel_id=1, source_target_pairs={{32,0},{36,4},{0,32},{4,36},{96,64},{100,68},{64,96},{68,100},{160... | collective-permute-start | bytes 73736 | tf_op jit(solution)/shard_map/ppermute | solution.py:33
  5.1 2.4 %collective-permute-start.2 = (f32[48,128]{1,0:T(8,128)S(1)}, f32[48,128]{1,0:T(8,128)S(1)}, u32[]{:S(2)}, u32[]{:S(2)}) collective-permute-start(f32[48,128]{1,0:T(8,128)S(1)} %maximum_maximum_fusion), channel_id=1, source_target_pairs={{36,0},{32,4},{4,32},{0,36},{100,64},{96,68},{68,96},{64,100},{164... | collective-permute-start | bytes 73736 | tf_op jit(solution)/shard_map/ppermute | solution.py:33
  7.5 6.1 %collective-permute-start.9 = (f32[40,256]{1,0:T(8,128)S(1)}, f32[40,256]{1,0:T(8,128)S(1)}, u32[]{:S(2)}, u32[]{:S(2)}) collective-permute-start(f32[40,256]{1,0:T(8,128)S(1)} %bitcast.45), channel_id=1, source_target_pairs={{0,248},{4,252},{8,0},{12,4},{16,8},{20,12},{24,16},{28,20},{32,24... | collective-permute-start | bytes 122888 | tf_op jit(solution)/shard_map/ppermute | solution.py:25
  13.8 5.2 %collective-permute-start.6 = (f32[40,256]{1,0:T(8,128)S(1)}, f32[40,256]{1,0:T(8,128)S(1)}, u32[]{:S(2)}, u32[]{:S(2)}) collective-permute-start(f32[40,256]{1,0:T(8,128)S(1)} %bitcast.48), channel_id=1, source_target_pairs={{0,4},{4,0},{1,5},{5,1},{2,6},{6,2},{3,7},{7,3},{8,12},{12,8},{9,1... | collective-permute-start | bytes 122888 | tf_op jit(solution)/shard_map/ppermute | solution.py:61
  19.8 3.1 %collective-permute-start.3 = (f32[48,128]{1,0:T(8,128)S(1)}, f32[48,128]{1,0:T(8,128)S(1)}, u32[]{:S(2)}, u32[]{:S(2)}) collective-permute-start(f32[48,128]{1,0:T(8,128)S(1)} %add_add_fusion.1), channel_id=1, source_target_pairs={{224,0},{64,32},{32,64},{128,96},{96,128},{192,160},{160,192},{0,2... | collective-permute-start | bytes 73736 | tf_op jit(solution)/shard_map/ppermute | solution.py:33
  25.4 12.7 %all_to_all.26.refs_0_ = f32[16,48,128]{2,1,0:T(8,128)S(1)} all-to-all(f32[16,48,128]{2,1,0:T(8,128)S(1)} %broadcast_in_dim.120), channel_id=1, replica_groups=mesh['agents_0'=8,'agents_1'=4,'agents_2'=2,'group'=4] {'agents_1','group'}, dimensions={0} | all-to-all | bytes 786432 | tf_op jit(solution)/shard_map/all_to_all | solution.py:53
  39.6 2.6 %collective-permute-start.13 = (f32[40,256]{1,0:T(8,128)S(1)}, f32[40,256]{1,0:T(8,128)S(1)}, u32[]{:S(2)}, u32[]{:S(2)}) collective-permute-start(f32[40,256]{1,0:T(8,128)S(1)} %get-tuple-element.32.own.refs_9_), channel_id=1, source_target_pairs={{0,248},{4,252},{8,0},{12,4},{16,8},{20,12},{24,16},{28,20},{32,24... | collective-permute-start | bytes 122888 | tf_op jit(solution)/shard_map/ppermute | solution.py:25
  42.3 2.6 %collective-permute-start.11 = (f32[40,256]{1,0:T(8,128)S(1)}, f32[40,256]{1,0:T(8,128)S(1)}, u32[]{:S(2)}, u32[]{:S(2)}) collective-permute-start(f32[40,256]{1,0:T(8,128)S(1)} %get-tuple-element.32.own.refs_9_), channel_id=1, source_target_pairs={{0,252},{4,8},{8,4},{12,16},{16,12},{20,24},{24,20},{28,32},{32,28... | collective-permute-start | bytes 122888 | tf_op jit(solution)/shard_map/ppermute | solution.py:62
  44.8 2.6 %collective-permute-start.10 = (f32[40,256]{1,0:T(8,128)S(1)}, f32[40,256]{1,0:T(8,128)S(1)}, u32[]{:S(2)}, u32[]{:S(2)}) collective-permute-start(f32[40,256]{1,0:T(8,128)S(1)} %get-tuple-element.32.own.refs_9_), channel_id=1, source_target_pairs={{0,4},{4,0},{1,5},{5,1},{2,6},{6,2},{3,7},{7,3},{8,12},{12,8},{9,1... | collective-permute-start | bytes 122888 | tf_op jit(solution)/shard_map/ppermute | solution.py:61
  49.9 6.3 %collective-permute-start.16 = (f32[40,128]{1,0:T(8,128)S(1)}, f32[40,128]{1,0:T(8,128)S(1)}, u32[]{:S(2)}, u32[]{:S(2)}) collective-permute-start(f32[40,128]{1,0:T(8,128)S(1)} %broadcast_select_fusion.1), channel_id=1, source_target_pairs={{36,0},{32,4},{4,32},{0,36},{100,64},{96,68},{68,96},{64,100},{164... | collective-permute-start | bytes 61448 | tf_op jit(solution)/shard_map/ppermute | solution.py:33
  58.0 2.1 %collective-permute-start.19 = (f32[40,128]{1,0:T(8,128)S(1)}, f32[40,128]{1,0:T(8,128)S(1)}, u32[]{:S(2)}, u32[]{:S(2)}) collective-permute-start(f32[40,128]{1,0:T(8,128)S(1)} %add_select_fusion.3), channel_id=1, source_target_pairs={{160,0},{128,32},{224,64},{192,96},{32,128},{0,160},{96,192},{64,2... | collective-permute-start | bytes 61448 | tf_op jit(solution)/shard_map/ppermute | solution.py:33
  60.7 3.5 %collective-permute-start.17 = (f32[40,128]{1,0:T(8,128)S(1)}, f32[40,128]{1,0:T(8,128)S(1)}, u32[]{:S(2)}, u32[]{:S(2)}) collective-permute-start(f32[40,128]{1,0:T(8,128)S(1)} %add_select_fusion.3), channel_id=1, source_target_pairs={{224,0},{64,32},{32,64},{128,96},{96,128},{192,160},{160,192},{0,2... | collective-permute-start | bytes 61448 | tf_op jit(solution)/shard_map/ppermute | solution.py:33
  65.6 10.3 %all_to_all.27.refs_0_ = f32[16,40,128]{2,1,0:T(8,128)S(1)} all-to-all(f32[16,40,128]{2,1,0:T(8,128)S(1)} %broadcast_in_dim.124), channel_id=1, replica_groups=mesh['agents_0'=8,'agents_1'=4,'agents_2'=2,'group'=4] {'agents_1','group'}, dimensions={0} | all-to-all | bytes 655360 | tf_op jit(solution)/shard_map/all_to_all | solution.py:53
  77.4 3.0 %collective-permute-start.23 = (f32[40,256]{1,0:T(8,128)S(1)}, f32[40,256]{1,0:T(8,128)S(1)}, u32[]{:S(2)}, u32[]{:S(2)}) collective-permute-start(f32[40,256]{1,0:T(8,128)S(1)} %get-tuple-element.37.own.refs_9_), channel_id=1, source_target_pairs={{0,248},{4,252},{8,0},{12,4},{16,8},{20,12},{24,16},{28,20},{32,24... | collective-permute-start | bytes 122888 | tf_op jit(solution)/shard_map/ppermute | solution.py:25
  80.4 2.3 %collective-permute-start.21 = (f32[40,256]{1,0:T(8,128)S(1)}, f32[40,256]{1,0:T(8,128)S(1)}, u32[]{:S(2)}, u32[]{:S(2)}) collective-permute-start(f32[40,256]{1,0:T(8,128)S(1)} %get-tuple-element.37.own.refs_9_), channel_id=1, source_target_pairs={{0,252},{4,8},{8,4},{12,16},{16,12},{20,24},{24,20},{28,32},{32,28... | collective-permute-start | bytes 122888 | tf_op jit(solution)/shard_map/ppermute | solution.py:62
  82.7 2.8 %collective-permute-start.20 = (f32[40,256]{1,0:T(8,128)S(1)}, f32[40,256]{1,0:T(8,128)S(1)}, u32[]{:S(2)}, u32[]{:S(2)}) collective-permute-start(f32[40,256]{1,0:T(8,128)S(1)} %get-tuple-element.37.own.refs_9_), channel_id=1, source_target_pairs={{0,4},{4,0},{1,5},{5,1},{2,6},{6,2},{3,7},{7,3},{8,12},{12,8},{9,1... | collective-permute-start | bytes 122888 | tf_op jit(solution)/shard_map/ppermute | solution.py:61
  87.8 6.3 %collective-permute-start.26 = (f32[40,128]{1,0:T(8,128)S(1)}, f32[40,128]{1,0:T(8,128)S(1)}, u32[]{:S(2)}, u32[]{:S(2)}) collective-permute-start(f32[40,128]{1,0:T(8,128)S(1)} %broadcast_select_fusion), channel_id=1, source_target_pairs={{36,0},{32,4},{4,32},{0,36},{100,64},{96,68},{68,96},{64,100},{164... | collective-permute-start | bytes 61448 | tf_op jit(solution)/shard_map/ppermute | solution.py:33
  94.1 1.7 %collective-permute-done.26 = f32[40,128]{1,0:T(8,128)S(1)} collective-permute-done((f32[40,128]{1,0:T(8,128)S(1)}, f32[40,128]{1,0:T(8,128)S(1)}, u32[]{:S(2)}, u32[]{:S(2)}) %collective-permute-start.26) | collective-permute-done | bytes 20512 | tf_op jit(solution)/shard_map/ppermute | solution.py:33
  97.7 2.9 %collective-permute-start.27 = (f32[40,128]{1,0:T(8,128)S(1)}, f32[40,128]{1,0:T(8,128)S(1)}, u32[]{:S(2)}, u32[]{:S(2)}) collective-permute-start(f32[40,128]{1,0:T(8,128)S(1)} %add_select_fusion.1), channel_id=1, source_target_pairs={{224,0},{64,32},{32,64},{128,96},{96,128},{192,160},{160,192},{0,2... | collective-permute-start | bytes 61448 | tf_op jit(solution)/shard_map/ppermute | solution.py:33
  102.4 10.5 %all_to_all.28.refs_0_ = f32[16,40,128]{2,1,0:T(8,128)S(1)} all-to-all(f32[16,40,128]{2,1,0:T(8,128)S(1)} %broadcast_in_dim.127), channel_id=1, replica_groups=mesh['agents_0'=8,'agents_1'=4,'agents_2'=2,'group'=4] {'agents_1','group'}, dimensions={0} | all-to-all | bytes 655360 | tf_op jit(solution)/shard_map/all_to_all | solution.py:53
  114.6 2.5 %collective-permute-start.33 = (f32[40,256]{1,0:T(8,128)S(1)}, f32[40,256]{1,0:T(8,128)S(1)}, u32[]{:S(2)}, u32[]{:S(2)}) collective-permute-start(f32[40,256]{1,0:T(8,128)S(1)} %get-tuple-element.43.own), channel_id=1, source_target_pairs={{0,248},{4,252},{8,0},{12,4},{16,8},{20,12},{24,16},{28,20},{32,24... | collective-permute-start | bytes 122888 | tf_op jit(solution)/shard_map/ppermute | solution.py:25
  117.0 2.8 %collective-permute-start.31 = (f32[40,256]{1,0:T(8,128)S(1)}, f32[40,256]{1,0:T(8,128)S(1)}, u32[]{:S(2)}, u32[]{:S(2)}) collective-permute-start(f32[40,256]{1,0:T(8,128)S(1)} %get-tuple-element.43.own), channel_id=1, source_target_pairs={{0,252},{4,8},{8,4},{12,16},{16,12},{20,24},{24,20},{28,32},{32,28... | collective-permute-start | bytes 122888 | tf_op jit(solution)/shard_map/ppermute | solution.py:62
  119.9 2.3 %collective-permute-start.30 = (f32[40,256]{1,0:T(8,128)S(1)}, f32[40,256]{1,0:T(8,128)S(1)}, u32[]{:S(2)}, u32[]{:S(2)}) collective-permute-start(f32[40,256]{1,0:T(8,128)S(1)} %get-tuple-element.43.own), channel_id=1, source_target_pairs={{0,4},{4,0},{1,5},{5,1},{2,6},{6,2},{3,7},{7,3},{8,12},{12,8},{9,1... | collective-permute-start | bytes 122888 | tf_op jit(solution)/shard_map/ppermute | solution.py:61
  124.8 23.6 %all_to_all.29 = f32[256,1,128]{2,1,0:T(1,128)S(1)} all-to-all(f32[256,1,128]{2,1,0:T(1,128)S(1)} %bitcast.58), channel_id=1, replica_groups=mesh['agents_0'=8,'agents_1'=4,'agents_2'=2,'group'=4] {'agents_0','agen..., dimensions={0} | all-to-all | bytes 262144 | tf_op jit(solution)/shard_map/all_to_all | solution.py:239
  (98 shorter events, 25.7 us)
Async XLA Ops:
  2.7 11.0 %collective-permute-start.1 = (f32[48,128]{1,0:T(8,128)S(1)}, f32[48,128]{1,0:T(8,128)S(1)}, u32[]{:S(2)}, u32[]{:S(2)}) collective-permute-start(f32[48,128]{1,0:T(8,128)S(1)} %maximum_maximum_fusion), channel_id=1, source_target_pairs={{32,0},{36,4},{0,32},{4,36},{96,64},{100,68},{64,96},{68,100},{160... | collective-permute-start | bytes 73736 | tf_op jit(solution)/shard_map/ppermute | solution.py:33
  5.1 8.6 %collective-permute-start.2 = (f32[48,128]{1,0:T(8,128)S(1)}, f32[48,128]{1,0:T(8,128)S(1)}, u32[]{:S(2)}, u32[]{:S(2)}) collective-permute-start(f32[48,128]{1,0:T(8,128)S(1)} %maximum_maximum_fusion), channel_id=1, source_target_pairs={{36,0},{32,4},{4,32},{0,36},{100,64},{96,68},{68,96},{64,100},{164... | collective-permute-start | bytes 73736 | tf_op jit(solution)/shard_map/ppermute | solution.py:33
  7.5 11.4 %collective-permute-start = (f32[48,128]{1,0:T(8,128)S(1)}, f32[48,128]{1,0:T(8,128)S(1)}, u32[]{:S(2)}, u32[]{:S(2)}) collective-permute-start(f32[48,128]{1,0:T(8,128)S(1)} %maximum_maximum_fusion), channel_id=1, source_target_pairs={{4,0},{0,4},{36,32},{32,36},{68,64},{64,68},{100,96},{96,100},{132... | collective-permute-start | bytes 73736 | tf_op jit(solution)/shard_map/ppermute | solution.py:33
  7.5 11.9 %collective-permute-start.9 = (f32[40,256]{1,0:T(8,128)S(1)}, f32[40,256]{1,0:T(8,128)S(1)}, u32[]{:S(2)}, u32[]{:S(2)}) collective-permute-start(f32[40,256]{1,0:T(8,128)S(1)} %bitcast.45), channel_id=1, source_target_pairs={{0,248},{4,252},{8,0},{12,4},{16,8},{20,12},{24,16},{28,20},{32,24... | collective-permute-start | bytes 122888 | tf_op jit(solution)/shard_map/ppermute | solution.py:25
  13.6 6.2 %collective-permute-start.8 = (f32[40,256]{1,0:T(8,128)S(1)}, f32[40,256]{1,0:T(8,128)S(1)}, u32[]{:S(2)}, u32[]{:S(2)}) collective-permute-start(f32[40,256]{1,0:T(8,128)S(1)} %bitcast.46), channel_id=1, source_target_pairs={{0,8},{4,12},{8,16},{12,20},{16,24},{20,28},{24,32},{28,36},{32,40... | collective-permute-start | bytes 122888 | tf_op jit(solution)/shard_map/ppermute | solution.py:25
  13.6 10.3 %collective-permute-start.7 = (f32[40,256]{1,0:T(8,128)S(1)}, f32[40,256]{1,0:T(8,128)S(1)}, u32[]{:S(2)}, u32[]{:S(2)}) collective-permute-start(f32[40,256]{1,0:T(8,128)S(1)} %bitcast.47), channel_id=1, source_target_pairs={{0,252},{4,8},{8,4},{12,16},{16,12},{20,24},{24,20},{28,32},{32,28... | collective-permute-start | bytes 122888 | tf_op jit(solution)/shard_map/ppermute | solution.py:62
  13.8 10.2 %collective-permute-start.6 = (f32[40,256]{1,0:T(8,128)S(1)}, f32[40,256]{1,0:T(8,128)S(1)}, u32[]{:S(2)}, u32[]{:S(2)}) collective-permute-start(f32[40,256]{1,0:T(8,128)S(1)} %bitcast.48), channel_id=1, source_target_pairs={{0,4},{4,0},{1,5},{5,1},{2,6},{6,2},{3,7},{7,3},{8,12},{12,8},{9,1... | collective-permute-start | bytes 122888 | tf_op jit(solution)/shard_map/ppermute | solution.py:61
  19.0 6.3 %collective-permute-start.5 = (f32[48,128]{1,0:T(8,128)S(1)}, f32[48,128]{1,0:T(8,128)S(1)}, u32[]{:S(2)}, u32[]{:S(2)}) collective-permute-start(f32[48,128]{1,0:T(8,128)S(1)} %add_add_fusion.1), channel_id=1, source_target_pairs={{160,0},{128,32},{224,64},{192,96},{32,128},{0,160},{96,192},{64,2... | collective-permute-start | bytes 73736 | tf_op jit(solution)/shard_map/ppermute | solution.py:33
  19.5 5.9 %collective-permute-start.4 = (f32[48,128]{1,0:T(8,128)S(1)}, f32[48,128]{1,0:T(8,128)S(1)}, u32[]{:S(2)}, u32[]{:S(2)}) collective-permute-start(f32[48,128]{1,0:T(8,128)S(1)} %add_add_fusion.1), channel_id=1, source_target_pairs={{64,0},{224,32},{128,64},{32,96},{192,128},{96,160},{0,192},{160,2... | collective-permute-start | bytes 73736 | tf_op jit(solution)/shard_map/ppermute | solution.py:33
  39.6 7.8 %collective-permute-start.13 = (f32[40,256]{1,0:T(8,128)S(1)}, f32[40,256]{1,0:T(8,128)S(1)}, u32[]{:S(2)}, u32[]{:S(2)}) collective-permute-start(f32[40,256]{1,0:T(8,128)S(1)} %get-tuple-element.32.own.refs_9_), channel_id=1, source_target_pairs={{0,248},{4,252},{8,0},{12,4},{16,8},{20,12},{24,16},{28,20},{32,24... | collective-permute-start | bytes 122888 | tf_op jit(solution)/shard_map/ppermute | solution.py:25
  42.3 6.2 %collective-permute-start.12 = (f32[40,256]{1,0:T(8,128)S(1)}, f32[40,256]{1,0:T(8,128)S(1)}, u32[]{:S(2)}, u32[]{:S(2)}) collective-permute-start(f32[40,256]{1,0:T(8,128)S(1)} %get-tuple-element.32.own.refs_9_), channel_id=1, source_target_pairs={{0,8},{4,12},{8,16},{12,20},{16,24},{20,28},{24,32},{28,36},{32,40... | collective-permute-start | bytes 122888 | tf_op jit(solution)/shard_map/ppermute | solution.py:25
  42.3 6.2 %collective-permute-start.11 = (f32[40,256]{1,0:T(8,128)S(1)}, f32[40,256]{1,0:T(8,128)S(1)}, u32[]{:S(2)}, u32[]{:S(2)}) collective-permute-start(f32[40,256]{1,0:T(8,128)S(1)} %get-tuple-element.32.own.refs_9_), channel_id=1, source_target_pairs={{0,252},{4,8},{8,4},{12,16},{16,12},{20,24},{24,20},{28,32},{32,28... | collective-permute-start | bytes 122888 | tf_op jit(solution)/shard_map/ppermute | solution.py:62
  49.6 6.6 %collective-permute-start.15 = (f32[40,128]{1,0:T(8,128)S(1)}, f32[40,128]{1,0:T(8,128)S(1)}, u32[]{:S(2)}, u32[]{:S(2)}) collective-permute-start(f32[40,128]{1,0:T(8,128)S(1)} %broadcast_select_fusion.1), channel_id=1, source_target_pairs={{32,0},{36,4},{0,32},{4,36},{96,64},{100,68},{64,96},{68,100},{160... | collective-permute-start | bytes 61448 | tf_op jit(solution)/shard_map/ppermute | solution.py:33
  49.9 8.1 %collective-permute-start.16 = (f32[40,128]{1,0:T(8,128)S(1)}, f32[40,128]{1,0:T(8,128)S(1)}, u32[]{:S(2)}, u32[]{:S(2)}) collective-permute-start(f32[40,128]{1,0:T(8,128)S(1)} %broadcast_select_fusion.1), channel_id=1, source_target_pairs={{36,0},{32,4},{4,32},{0,36},{100,64},{96,68},{68,96},{64,100},{164... | collective-permute-start | bytes 61448 | tf_op jit(solution)/shard_map/ppermute | solution.py:33
  58.0 6.2 %collective-permute-start.19 = (f32[40,128]{1,0:T(8,128)S(1)}, f32[40,128]{1,0:T(8,128)S(1)}, u32[]{:S(2)}, u32[]{:S(2)}) collective-permute-start(f32[40,128]{1,0:T(8,128)S(1)} %add_select_fusion.3), channel_id=1, source_target_pairs={{160,0},{128,32},{224,64},{192,96},{32,128},{0,160},{96,192},{64,2... | collective-permute-start | bytes 61448 | tf_op jit(solution)/shard_map/ppermute | solution.py:33
  77.4 8.1 %collective-permute-start.23 = (f32[40,256]{1,0:T(8,128)S(1)}, f32[40,256]{1,0:T(8,128)S(1)}, u32[]{:S(2)}, u32[]{:S(2)}) collective-permute-start(f32[40,256]{1,0:T(8,128)S(1)} %get-tuple-element.37.own.refs_9_), channel_id=1, source_target_pairs={{0,248},{4,252},{8,0},{12,4},{16,8},{20,12},{24,16},{28,20},{32,24... | collective-permute-start | bytes 122888 | tf_op jit(solution)/shard_map/ppermute | solution.py:25
  80.4 6.2 %collective-permute-start.22 = (f32[40,256]{1,0:T(8,128)S(1)}, f32[40,256]{1,0:T(8,128)S(1)}, u32[]{:S(2)}, u32[]{:S(2)}) collective-permute-start(f32[40,256]{1,0:T(8,128)S(1)} %get-tuple-element.37.own.refs_9_), channel_id=1, source_target_pairs={{0,8},{4,12},{8,16},{12,20},{16,24},{20,28},{24,32},{28,36},{32,40... | collective-permute-start | bytes 122888 | tf_op jit(solution)/shard_map/ppermute | solution.py:25
  80.4 6.2 %collective-permute-start.21 = (f32[40,256]{1,0:T(8,128)S(1)}, f32[40,256]{1,0:T(8,128)S(1)}, u32[]{:S(2)}, u32[]{:S(2)}) collective-permute-start(f32[40,256]{1,0:T(8,128)S(1)} %get-tuple-element.37.own.refs_9_), channel_id=1, source_target_pairs={{0,252},{4,8},{8,4},{12,16},{16,12},{20,24},{24,20},{28,32},{32,28... | collective-permute-start | bytes 122888 | tf_op jit(solution)/shard_map/ppermute | solution.py:62
  87.7 6.4 %collective-permute-start.25 = (f32[40,128]{1,0:T(8,128)S(1)}, f32[40,128]{1,0:T(8,128)S(1)}, u32[]{:S(2)}, u32[]{:S(2)}) collective-permute-start(f32[40,128]{1,0:T(8,128)S(1)} %broadcast_select_fusion), channel_id=1, source_target_pairs={{32,0},{36,4},{0,32},{4,36},{96,64},{100,68},{64,96},{68,100},{160... | collective-permute-start | bytes 61448 | tf_op jit(solution)/shard_map/ppermute | solution.py:33
  87.8 8.1 %collective-permute-start.26 = (f32[40,128]{1,0:T(8,128)S(1)}, f32[40,128]{1,0:T(8,128)S(1)}, u32[]{:S(2)}, u32[]{:S(2)}) collective-permute-start(f32[40,128]{1,0:T(8,128)S(1)} %broadcast_select_fusion), channel_id=1, source_target_pairs={{36,0},{32,4},{4,32},{0,36},{100,64},{96,68},{68,96},{64,100},{164... | collective-permute-start | bytes 61448 | tf_op jit(solution)/shard_map/ppermute | solution.py:33
  95.9 5.7 %collective-permute-start.29 = (f32[40,128]{1,0:T(8,128)S(1)}, f32[40,128]{1,0:T(8,128)S(1)}, u32[]{:S(2)}, u32[]{:S(2)}) collective-permute-start(f32[40,128]{1,0:T(8,128)S(1)} %add_select_fusion.1), channel_id=1, source_target_pairs={{160,0},{128,32},{224,64},{192,96},{32,128},{0,160},{96,192},{64,2... | collective-permute-start | bytes 61448 | tf_op jit(solution)/shard_map/ppermute | solution.py:33
  114.6 7.7 %collective-permute-start.33 = (f32[40,256]{1,0:T(8,128)S(1)}, f32[40,256]{1,0:T(8,128)S(1)}, u32[]{:S(2)}, u32[]{:S(2)}) collective-permute-start(f32[40,256]{1,0:T(8,128)S(1)} %get-tuple-element.43.own), channel_id=1, source_target_pairs={{0,248},{4,252},{8,0},{12,4},{16,8},{20,12},{24,16},{28,20},{32,24... | collective-permute-start | bytes 122888 | tf_op jit(solution)/shard_map/ppermute | solution.py:25
  117.0 6.2 %collective-permute-start.32 = (f32[40,256]{1,0:T(8,128)S(1)}, f32[40,256]{1,0:T(8,128)S(1)}, u32[]{:S(2)}, u32[]{:S(2)}) collective-permute-start(f32[40,256]{1,0:T(8,128)S(1)} %get-tuple-element.43.own), channel_id=1, source_target_pairs={{0,8},{4,12},{8,16},{12,20},{16,24},{20,28},{24,32},{28,36},{32,40... | collective-permute-start | bytes 122888 | tf_op jit(solution)/shard_map/ppermute | solution.py:25
  117.0 6.2 %collective-permute-start.31 = (f32[40,256]{1,0:T(8,128)S(1)}, f32[40,256]{1,0:T(8,128)S(1)}, u32[]{:S(2)}, u32[]{:S(2)}) collective-permute-start(f32[40,256]{1,0:T(8,128)S(1)} %get-tuple-element.43.own), channel_id=1, source_target_pairs={{0,252},{4,8},{8,4},{12,16},{16,12},{20,24},{24,20},{28,32},{32,28... | collective-permute-start | bytes 122888 | tf_op jit(solution)/shard_map/ppermute | solution.py:62
  (19 other events, 141.8 us)
